TPU v7x, 32 devices: a whole 2x2x4 slice. The times are simulated.
32 devices in a mesh: energy: 2 (over y), slab: 4 (over z), orb: 2 (over x), rhs: 2 (over core).
Axes of the slice: x: 2, y: 2, z: 4, core: 2. Of those that a mesh axis runs over, the one named last changes fastest.
Arguments:
- diag_blocks: float32 [16, 192, 384], P(('energy', 'slab'), 'orb'), parts along dimension 0, may hold values from -8 to 8, as said below
- couplings: float32 [16, 192, 384], P(('energy', 'slab')), parts along dimension 0, may hold values from -8 to 8
- sources: float32 [16, 32, 384], P(('energy', 'slab'), ('orb', 'rhs')), parts along dimension 0, may hold values from -8 to 8
Outputs:
- solution: float32 [16, 32, 384], P(('energy', 'slab'), ('orb', 'rhs')), parts along dimension 0
There are 2 independent parts, one for each index of `energy`. A program takes and returns all parts, laid end to end along the dimension named above; each array names one. Nothing has to cross between parts.
Inputs may be any that keep to these rules, and one draw needn't show every extreme that they name: Every diag_blocks[n] is Hermitian, and together with couplings it makes K positive definite with smallest eigenvalue 0.01 or more.
All inputs are finite; a program needn't handle non-finite values.
Results may differ from a plain program's by a relative error of at most 0.0003.
Values sent between devices are 32-bit elements; how exact they have to be, the bound alone decides.
A program may use at most 128 MiB of HBM per device.

v0:
```python
import jax
import jax.numpy as jnp
from jax import lax
from jax.sharding import PartitionSpec as P
from jax.experimental import pallas as pl
from jax.experimental.pallas import tpu as pltpu

HALF = 64
LANES = 2 * HALF


def dot(left, right, dims=((1,), (0,))):
    return lax.dot_general(
        left,
        right,
        (dims, ((), ())),
        precision=lax.Precision.HIGHEST,
        preferred_element_type=jnp.float32,
    )


def dot_flipped(left, right):
    return dot(left, right, ((1,), (1,)))


def lane_sign(shape):
    lane = lax.broadcasted_iota(jnp.int32, shape, 1)
    return jnp.where(lane % LANES < HALF, -1.0, 1.0).astype(jnp.float32)


def times_i(rows):
    pieces = [
        pltpu.roll(rows[:, start : start + LANES], HALF, 1)
        for start in range(0, rows.shape[1], LANES)
    ]
    turned = pieces[0] if len(pieces) == 1 else jnp.concatenate(pieces, axis=1)
    return turned * lane_sign(turned.shape)


def interleave(rows):
    count = rows.shape[1] // LANES
    pieces = []
    for chunk in range(count):
        pieces.append(rows[:, chunk * HALF : (chunk + 1) * HALF])
        pieces.append(rows[:, (count + chunk) * HALF : (count + chunk + 1) * HALF])
    return jnp.concatenate(pieces, axis=1)


def separate(rows):
    count = rows.shape[1] // LANES
    pieces = [rows[:, 2 * chunk * HALF : (2 * chunk + 1) * HALF] for chunk in range(count)]
    pieces += [rows[:, (2 * chunk + 1) * HALF : (2 * chunk + 2) * HALF] for chunk in range(count)]
    return jnp.concatenate(pieces, axis=1)


def embed(rows):
    turned = times_i(rows)
    pieces = []
    for start in range(0, rows.shape[0], HALF):
        pieces += [rows[start : start + HALF], turned[start : start + HALF]]
    return jnp.concatenate(pieces, axis=0)


def compact(embedded):
    return jnp.concatenate(
        [embedded[start : start + HALF] for start in range(0, embedded.shape[0], LANES)], axis=0
    )


GROUP = 16
TALL = 8


def product(left, right):
    return (left[0] * right[0] - left[1] * right[1], left[0] * right[1] + left[1] * right[0])


def conjugate(value):
    return (value[0], -value[1])


def plus(left, right):
    return (left[0] + right[0], left[1] + right[1])


def minus(left, right):
    return (left[0] - right[0], left[1] - right[1])


def squared(value):
    return value[0] * value[0] + value[1] * value[1]


def scaled_by(value, factor):
    return (value[0] * factor, value[1] * factor)


def invert_pair(head, cross, tail):
    scale = 1.0 / (head * tail - squared(cross))
    return tail * scale, scaled_by(cross, -scale), head * scale


def invert_four(at):
    head = invert_pair(at[0][0][0], at[0][1], at[1][1][0])
    upper = [[at[0][2], at[0][3]], [at[1][2], at[1][3]]]
    mixed = [
        [plus(scaled_by(upper[0][j], head[0]), product(head[1], upper[1][j])) for j in range(2)],
        [
            plus(product(conjugate(head[1]), upper[0][j]), scaled_by(upper[1][j], head[2]))
            for j in range(2)
        ],
    ]

    def schur(i, j):
        return plus(
            product(conjugate(upper[0][i]), mixed[0][j]),
            product(conjugate(upper[1][i]), mixed[1][j]),
        )

    tail = invert_pair(
        at[2][2][0] - schur(0, 0)[0],
        minus(at[2][3], schur(0, 1)),
        at[3][3][0] - schur(1, 1)[0],
    )
    carried = [
        [
            plus(scaled_by(mixed[i][0], tail[0]), product(mixed[i][1], conjugate(tail[1]))),
            plus(product(mixed[i][0], tail[1]), scaled_by(mixed[i][1], tail[2])),
        ]
        for i in range(2)
    ]

    def corner(i, j):
        return plus(
            product(carried[i][0], conjugate(mixed[j][0])),
            product(carried[i][1], conjugate(mixed[j][1])),
        )

    zero = jnp.zeros_like(head[0])
    result = [[None] * 4 for _ in range(4)]
    result[0][0] = (head[0] + corner(0, 0)[0], zero)
    result[0][1] = plus(head[1], corner(0, 1))
    result[1][1] = (head[2] + corner(1, 1)[0], zero)
    result[2][2], result[2][3], result[3][3] = (tail[0], zero), tail[1], (tail[2], zero)
    for i in range(2):
        for j in range(2):
            result[i][2 + j] = (-carried[i][j][0], -carried[i][j][1])
    for i in range(4):
        for j in range(i):
            result[i][j] = conjugate(result[j][i])
    return result


def spread_row(rows, at):
    return jnp.broadcast_to(rows[at : at + 1], (TALL, LANES))


def spread_lane(rows, at):
    return jnp.broadcast_to(rows[:, at : at + 1], (TALL, LANES))


def invert_group(rows, first, sign, lane, row_id):
    parts = [rows[start : start + TALL] for start in range(0, GROUP, TALL)]
    for offset in range(0, GROUP, 4):
        step = first + offset
        home, inner = divmod(offset, TALL)
        columns = [
            [(spread_lane(part, step + at), spread_lane(part, step + at + HALF)) for at in range(4)]
            for part in parts
        ]
        inverse = invert_four(
            [
                [
                    tuple(spread_row(value, inner + i) for value in columns[home][j])
                    if j >= i
                    else None
                    for j in range(4)
                ]
                for i in range(4)
            ]
        )
        inside = (lane % HALF >= step) & (lane % HALF < step + 4)
        cleared = jnp.where(inside, 0.0, parts[home])
        turned = pltpu.roll(cleared, HALF, 1) * sign
        plain, spun = [], []
        for at in range(4):
            plain.append(spread_row(cleared, inner + at) + jnp.where(lane == step + at, 1.0, 0.0))
            spun.append(
                spread_row(turned, inner + at) + jnp.where(lane == step + at + HALF, 1.0, 0.0)
            )
        new_rows, new_spins = [], []
        for i in range(4):
            new = spin = None
            for j in range(4):
                real, imag = inverse[i][j]
                if i == j:
                    term, turn = real * plain[j], real * spun[j]
                else:
                    term = real * plain[j] + imag * spun[j]
                    turn = real * spun[j] - imag * plain[j]
                new, spin = (term, turn) if new is None else (new + term, spin + turn)
            new_rows.append(new)
            new_spins.append(spin)
        updated = []
        for index, part in enumerate(parts):
            fresh = jnp.where(inside, 0.0, part)
            for i in range(4):
                real, imag = columns[index][i]
                fresh = fresh - (real * new_rows[i] + imag * new_spins[i])
            if index == home:
                for i in range(4):
                    fresh = jnp.where(row_id == inner + i, new_rows[i], fresh)
            updated.append(fresh)
        parts = updated
    return jnp.concatenate(parts, axis=0) if len(parts) > 1 else parts[0]


def spread_out(done, spun, first):
    last = HALF - first - GROUP
    before = [jnp.zeros((first, LANES), jnp.float32)] if first else []
    after = [jnp.zeros((last, LANES), jnp.float32)] if last else []
    return jnp.concatenate(before + [done] + after + before + [spun] + after, axis=0)


def invert_small(block):
    lane = lax.broadcasted_iota(jnp.int32, (1, LANES), 1)
    row_id = lax.broadcasted_iota(jnp.int32, (TALL, 1), 0)
    sign = lane_sign((1, LANES))
    group = block[:GROUP]
    for first in range(0, HALF, GROUP):
        done = invert_group(group, first, sign, lane, row_id)
        spun = pltpu.roll(done, HALF, 1) * sign
        inside = (lane % HALF >= first) & (lane % HALF < first + GROUP)
        following = first + GROUP
        if following < HALF:
            old = block[following : following + GROUP]
            group = jnp.where(inside, 0.0, old)
            for at in range(GROUP):
                group = group - (
                    old[:, first + at : first + at + 1] * done[at : at + 1]
                    + old[:, first + at + HALF : first + at + HALF + 1] * spun[at : at + 1]
                )
        rest = jnp.where(inside, 0.0, block) - dot(
            jnp.where(inside, block, 0.0), spread_out(done, spun, first)
        )
        above = [rest[:first]] if first else []
        below = [rest[following:]] if following < HALF else []
        block = jnp.concatenate(above + [done] + below, axis=0)
    return block


def invert(ref):
    order = ref.shape[0]

    def step(k, carry):
        rows = pl.ds(pl.multiple_of(k * HALF, HALF), HALF)
        lanes = pl.ds(pl.multiple_of(k * LANES, LANES), LANES)
        small = invert_small(ref[rows, lanes])
        panel = ref[rows, :]
        ref[rows, :] = dot(small, jnp.concatenate([panel, times_i(panel)], axis=0))
        ref[rows, lanes] = small
        fresh = ref[rows, :]
        column = ref[:, lanes]
        ref[:, lanes] = jnp.zeros((order, LANES), jnp.float32)
        ref[...] = ref[...] - dot(column, jnp.concatenate([fresh, times_i(fresh)], axis=0))
        ref[rows, :] = fresh
        return carry

    lax.fori_loop(0, order // HALF, step, 0)


def eliminate(pivot_ref, to_pivot_v, to_pivot_u, block_v, block_u, load_i, load_v, load_u):
    invert(pivot_ref)
    return apply_pivot(
        pivot_ref, to_pivot_v, to_pivot_u, block_v, block_u, load_i, load_v, load_u
    )


def apply_pivot(pivot_ref, to_pivot_v, to_pivot_u, block_v, block_u, load_i, load_v, load_u):
    order, rhs = block_v.shape[0], load_i.shape[0]
    inverse = embed(pivot_ref[...])
    stacked = [compact(to_pivot_v), load_i]
    if to_pivot_u is not None:
        stacked.append(compact(to_pivot_u))
    through = dot(jnp.concatenate(stacked, axis=0), inverse)
    toward_v = dot_flipped(through[: order + rhs], to_pivot_v)
    new_v = jnp.concatenate([block_v, load_v], axis=0) - toward_v
    kept = (through[:order], through[order : order + rhs])
    if to_pivot_u is None:
        return new_v, kept
    toward_u = dot_flipped(through, to_pivot_u)
    new_u = jnp.concatenate([block_u, load_u], axis=0) - jnp.concatenate(
        [toward_u[order + rhs :], toward_u[order : order + rhs]], axis=0
    )
    return new_v, new_u, -toward_u[:order], kept + (through[order + rhs :],)


def flip_where(flip, ref, embedded):
    @pl.when(flip)
    def _():
        ref[...] = embedded.T

    @pl.when(jnp.logical_not(flip))
    def _():
        ref[...] = embedded


def is_left():
    return lax.axis_index("slab") < lax.axis_size("slab") // 2


def invert_kernel(block, inverse):
    inverse[...] = interleave(block[...])
    invert(inverse)


def interior_kernel(
    inverse, boundary, inner, outer, loads,
    new_v, new_u, cross, kept_v, kept_b, kept_u, to_v, to_u,
):
    left = is_left()
    at_interior = jnp.where(left, 0, 1)
    flip_where(left, to_v, embed(interleave(inner[...])))
    flip_where(jnp.logical_not(left), to_u, embed(interleave(outer[...])))
    load_i = interleave(loads[at_interior])
    load_v = interleave(loads[1 - at_interior])
    block_v = interleave(boundary[...])
    zero = jnp.zeros_like(block_v)
    new_v[...], new_u[...], cross[...], kept = apply_pivot(
        inverse, to_v[...], to_u[...], block_v, zero, load_i, load_v, jnp.zeros_like(load_v)
    )
    kept_v[...], kept_b[...], kept_u[...] = kept


def level_kernel(own_v, own_u, own_cross, first_v, new_v, kept_v, kept_b, pivot):
    order = pivot.shape[0]
    joined = first_v[...] + own_u[...]
    pivot[...] = joined[:order]
    new_v[...], kept = eliminate(
        pivot, embed(own_cross[...]), None, own_v[:order], None, joined[order:], own_v[order:], None
    )
    kept_v[...], kept_b[...] = kept


def wide_level_kernel(
    own_v, own_u, own_cross, first_v, first_u, first_cross,
    new_v, new_u, cross, kept_v, kept_b, kept_u, pivot,
):
    order = pivot.shape[0]
    joined = first_v[...] + own_u[...]
    pivot[...] = joined[:order]
    new_v[...], new_u[...], cross[...], kept = eliminate(
        pivot,
        embed(own_cross[...]),
        embed(first_cross[...]).T,
        own_v[:order],
        first_u[:order],
        joined[order:],
        own_v[order:],
        first_u[order:],
    )
    kept_v[...], kept_b[...], kept_u[...] = kept


def center_kernel(own, other, coupling, value, pivot, to_other):
    order = pivot.shape[0]
    flip_where(jnp.logical_not(is_left()), to_other, embed(interleave(coupling[...])))
    pivot[...] = other[:order]
    reduced, _ = eliminate(
        pivot, to_other[...], None, own[:order], None, other[order:], own[order:], None
    )
    pivot[...] = reduced[:order]
    invert(pivot)
    value[...] = dot(reduced[order:], embed(pivot[...]))


def back_kernel(value_v, value_u, kept_v, kept_b, kept_u, middle):
    middle[...] = (
        kept_b[...]
        - dot(value_v[...], embed(kept_v[...]))
        - dot(value_u[...], embed(kept_u[...]))
    )


def narrow_back_kernel(value_v, kept_v, kept_b, middle):
    middle[...] = kept_b[...] - dot(value_v[...], embed(kept_v[...]))


def final_kernel(value_v, value_u, kept_v, kept_b, kept_u, result):
    middle = (
        kept_b[...]
        - dot(value_v[...], embed(kept_v[...]))
        - dot(value_u[...], embed(kept_u[...]))
    )
    at_interior = jnp.where(is_left(), 0, 1)
    result[at_interior] = separate(middle)
    result[1 - at_interior] = separate(value_v[...])


def call(kernel, outs, scratch, *operands, flops=0):
    return pl.pallas_call(
        kernel,
        out_shape=[jax.ShapeDtypeStruct(shape, jnp.float32) for shape in outs],
        scratch_shapes=[pltpu.VMEM(shape, jnp.float32) for shape in scratch],
        cost_estimate=pl.CostEstimate(flops=flops, bytes_accessed=flops // 64, transcendentals=0)
        if flops
        else None,
        compiler_params=pltpu.CompilerParams(vmem_limit_bytes=48 * 1024 * 1024),
    )(*operands)


def gather_columns(shard):
    size = lax.axis_size("orb")
    index = lax.axis_index("orb")
    distance = 1
    while distance < size:
        theirs = lax.ppermute(shard, "orb", [(i, i ^ distance) for i in range(size)])
        first = index // distance % 2 == 0
        shard = jnp.where(
            first,
            jnp.concatenate([shard, theirs], axis=0),
            jnp.concatenate([theirs, shard], axis=0),
        )
        distance *= 2
    return shard


def local(diag_blocks, couplings, sources):
    order, width = couplings.shape[1:]
    rhs = sources.shape[1]
    slabs = lax.axis_size("slab")
    half = slabs // 2
    slab = lax.axis_index("slab")
    left = slab < half
    place = jnp.where(left, slab, slabs - 1 - slab)

    def at(position):
        return (position, slabs - 1 - position)

    shifted = lax.ppermute(couplings[0], "slab", [(i, i - 1) for i in range(half, slabs)])
    interior = gather_columns(jnp.where(left, diag_blocks[0], diag_blocks[1]))
    held = jnp.where(left, diag_blocks[1], diag_blocks[0])
    interior, held = lax.optimization_barrier((interior, held))
    boundary = gather_columns(held)
    outer = jnp.where(left, jnp.where(slab > 0, couplings[0], 0.0), shifted)
    center = jnp.where(left, shifted, couplings[0])
    square, tall, thin, full = (order, width), (order + rhs, width), (rhs, width), (width, width)

    (inverse,) = call(invert_kernel, [square], [], interior, flops=64 * order * width * width)
    new_v, new_u, cross, kept_v, kept_b, kept_u = call(
        interior_kernel,
        [tall, tall, square, square, thin, square],
        [full, full],
        inverse, boundary, couplings[1], outer, sources,
    )
    levels = half.bit_length() - 1
    stored = []
    for level in range(levels):
        distance = 2**level
        firsts = range(distance - 1, half, 2 * distance)
        pairs = [
            (a, b) for first in firsts for a, b in zip(at(first), at(first + distance), strict=True)
        ]
        first_v = lax.ppermute(new_v, "slab", pairs)
        if level == levels - 1:
            new_v, level_v, level_b = call(
                level_kernel, [tall, square, thin], [square], new_v, new_u, cross, first_v
            )
            stored.append((distance, pairs, (level_v, level_b)))
        else:
            first_u = lax.ppermute(new_u, "slab", pairs)
            first_cross = lax.ppermute(cross, "slab", pairs)
            new_v, new_u, cross, level_v, level_b, level_u = call(
                wide_level_kernel,
                [tall, tall, square, square, thin, square],
                [square],
                new_v, new_u, cross, first_v, first_u, first_cross,
            )
            stored.append((distance, pairs, (level_v, level_b, level_u)))
    other = lax.ppermute(new_v, "slab", [(half - 1, half), (half, half - 1)])
    (value_v,) = call(center_kernel, [thin], [square, full], new_v, other, center)
    value_u = jnp.zeros_like(value_v)
    for distance, pairs, kept in reversed(stored):
        if len(kept) == 2:
            (middle,) = call(narrow_back_kernel, [thin], [], value_v, *kept)
        else:
            (middle,) = call(back_kernel, [thin], [], value_v, value_u, *kept)
        sent = lax.ppermute(
            jnp.concatenate([middle, value_u]), "slab", [(b, a) for a, b in pairs]
        )
        is_first = place % (2 * distance) == distance - 1
        value_v = jnp.where(is_first, sent[:rhs], value_v)
        value_u = jnp.where(is_first, sent[rhs:], middle)
    (result,) = call(
        final_kernel, [sources.shape], [], value_v, value_u, kept_v, kept_b, kept_u
    )
    return result


def solution(mesh):
    placed = (
        P(("energy", "slab"), "orb", None),
        P(("energy", "slab"), None, None),
        P(("energy", "slab"), ("orb", "rhs"), None),
    )
    return jax.shard_map(
        local,
        mesh=mesh,
        in_specs=placed,
        out_specs=P(("energy", "slab"), ("orb", "rhs"), None),
        check_vma=False,
    )
```

profile of v0, /device:TPU:0, one launch (start us, length us, event | category | flops | bytes accessed | tf_op | source)
XLA Modules:
  0.0 94.7 jit_solution(12694490978678072926)
XLA Ops:
  0.0 0.0 copy-start.1
  0.0 1.1 %select_bitcast_fusion = (f32[96,384]{1,0:T(8,128)S(1)}, f32[96,384]{1,0:T(8,128)S(1)}) fusion(f32[2,96,384]{2,1,0:T(8,128)} %param.3, pred[]{:T(512)S(6)} %lt.15), kind=kLoop, calls=%fused_computation.5 | loop fusion | flops 73728 | bytes 589825 | tf_op jit(solution)/shard_map/jit(_where)/select_n | solution.py:442
  1.1 3.0 %collective-permute-start = (f32[96,384]{1,0:T(8,128)S(1)}, f32[96,384]{1,0:T(8,128)S(1)}, u32[]{:S(2)}, u32[]{:S(2)}) collective-permute-start(f32[96,384]{1,0:T(8,128)S(1)} %get-tuple-element.32), channel_id=1, source_target_pairs={{0,2},{2,0},{1,3},{3,1},{4,6},{6,4},{5,7},{7,5},{8,10},{10,8},{9,1... | collective-permute-start | bytes 442376 | tf_op jit(solution)/shard_map/ppermute | solution.py:417
  4.1 0.0 copy-done.1
  4.1 0.7 collective-permute-start.2
  4.9 3.1 %collective-permute-done = f32[96,384]{1,0:T(8,128)S(1)} collective-permute-done((f32[96,384]{1,0:T(8,128)S(1)}, f32[96,384]{1,0:T(8,128)S(1)}, u32[]{:S(2)}, u32[]{:S(2)}) %collective-permute-start) | collective-permute-done | bytes 147488 | tf_op jit(solution)/shard_map/ppermute | solution.py:417
  8.0 1.8 %collective-permute-start.1 = (f32[96,384]{1,0:T(8,128)S(1)}, f32[96,384]{1,0:T(8,128)S(1)}, u32[]{:S(2)}, u32[]{:S(2)}) collective-permute-start(f32[96,384]{1,0:T(8,128)S(1)} %get-tuple-element.17), channel_id=1, source_target_pairs={{0,2},{2,0},{1,3},{3,1},{4,6},{6,4},{5,7},{7,5},{8,10},{10,8},{9,1... | collective-permute-start | bytes 442376 | tf_op jit(solution)/shard_map/ppermute | solution.py:417
  9.8 12.7 %shard_map.37.inverse = f32[192,384]{1,0:T(8,128)S(1)} custom-call(f32[192,384]{1,0:T(8,128)S(1)} %maximum_select_fusion.block), custom_call_target="tpu_custom_call" | custom-call | flops 1811939328 | bytes 28311552 | tf_op jit(solution)/shard_map/pallas_call | solution.py:401
  22.5 0.0 collective-permute-done.1
  22.6 0.0 copy-start
  22.6 0.0 collective-permute-done.2
  22.6 0.7 copy-done
  23.3 4.1 %shard_map.38 = (f32[200,384]{1,0:T(8,128)S(1)}, f32[200,384]{1,0:T(8,128)S(1)}, f32[192,384]{1,0:T(8,128)S(1)}, f32[192,384]{1,0:T(8,128)S(1)}, f32[8,384]{1,0:T(8,128)S(1)}, /*index=5*/f32[192,384]{1,0:T(8,128)S(1)}) custom-call(f32[192,384]{1,0:T(8,128)S(1)} %shard_map.37.inverse, f32[192,384]{1,0:T(8,128)S(1)} %maximum_select_fusion.1.boundary, ...), custom_call_target="tpu_custom_call" | custom-call | tf_op jit(solution)/shard_map/pallas_call | solution.py:401
  27.4 3.5 %collective-permute-start.3 = (f32[200,384]{1,0:T(8,128)S(1)}, f32[200,384]{1,0:T(8,128)S(1)}, u32[]{:S(2)}, u32[]{:S(2)}) collective-permute-start(f32[200,384]{1,0:T(8,128)S(1)} %get-tuple-element.18.own_v), channel_id=1, source_target_pairs={{0,4},{12,8},{1,5},{13,9},{2,6},{14,10},{3,7},{15,11},{16,20},{28,... | collective-permute-start | bytes 921608 | tf_op jit(solution)/shard_map/ppermute | solution.py:464
  30.9 5.4 %collective-permute-done.3.first_v = f32[200,384]{1,0:T(8,128)S(1)} collective-permute-done((f32[200,384]{1,0:T(8,128)S(1)}, f32[200,384]{1,0:T(8,128)S(1)}, u32[]{:S(2)}, u32[]{:S(2)}) %collective-permute-start.3) | collective-permute-done | bytes 307232 | tf_op jit(solution)/shard_map/ppermute | solution.py:464
  36.3 14.4 %shard_map.39 = (f32[200,384]{1,0:T(8,128)S(1)}, f32[192,384]{1,0:T(8,128)S(1)}, f32[8,384]{1,0:T(8,128)S(1)}) custom-call(f32[200,384]{1,0:T(8,128)S(1)} %get-tuple-element.18.own_v, f32[200,384]{1,0:T(8,128)S(1)} %get-tuple-element.19.own_u, f32[192,384]{1,0:T(8,128)S(1)} %get-tuple-element.20.own_cross, f32[200,384]{1,0:T(8,128)S(1)} %collective-permute-done.3.first_v), custom_call_target="tpu_custom_call" | custom-call | tf_op jit(solution)/shard_map/pallas_call | solution.py:401
  50.7 0.7 collective-permute-start.4
  51.3 0.0 collective-permute-done.4.other
  51.4 27.7 %shard_map.40.value_v = f32[8,384]{1,0:T(8,128)S(1)} custom-call(f32[200,384]{1,0:T(8,128)S(1)} %get-tuple-element.21.own, f32[200,384]{1,0:T(8,128)S(1)} %collective-permute-done.4.other, f32[192,384]{1,0:T(8,128)S(1)} %get-tuple-element.27.coupling), custom_call_target="tpu_custom_call" | custom-call | tf_op jit(solution)/shard_map/pallas_call | solution.py:401
  79.0 0.5 shard_map.41
  79.5 1.3 %collective-permute-start.5 = (f32[16,384]{1,0:T(8,128)S(1)}, f32[16,384]{1,0:T(8,128)S(1)}, u32[]{:S(2)}, u32[]{:S(2)}) collective-permute-start(f32[16,384]{1,0:T(8,128)S(1)} %concatenate.19), channel_id=1, source_target_pairs={{4,0},{8,12},{5,1},{9,13},{6,2},{10,14},{7,3},{11,15},{20,16},{24,... | collective-permute-start | bytes 73736 | tf_op jit(solution)/shard_map/ppermute | solution.py:488
  80.8 12.5 %collective-permute-done.5 = f32[16,384]{1,0:T(8,128)S(1)} collective-permute-done((f32[16,384]{1,0:T(8,128)S(1)}, f32[16,384]{1,0:T(8,128)S(1)}, u32[]{:S(2)}, u32[]{:S(2)}) %collective-permute-start.5) | collective-permute-done | bytes 24608 | tf_op jit(solution)/shard_map/ppermute | solution.py:488
  93.3 1.4 %shard_map.42 = f32[2,8,384]{2,1,0:T(8,128)} custom-call(f32[8,384]{1,0:T(8,128)S(1)} %get-tuple-element.34.value_v, f32[8,384]{1,0:T(8,128)S(1)} %get-tuple-element.33.value_u, f32[192,384]{1,0:T(8,128)S(1)} %get-tuple-element.24.kept_v, f32[8,384]{1,0:T(8,128)S(1)} %get-tuple-element.25.kept_b, f32[192,384]{1,0:T(8,128)S(1)} %get-tuple-element.26.kept_u), custom_call_target="tpu_custom_call" | custom-call | tf_op jit(solution)/shard_map/pallas_call | solution.py:401
  (6 shorter events, 0.1 us)
Async XLA Ops:
  0.0 4.1 %copy-start.1 = (f32[2,192,384]{2,1,0:T(8,128)S(1)}, f32[2,192,384]{2,1,0:T(8,128)}, u32[]{:S(2)}) copy-start(f32[2,192,384]{2,1,0:T(8,128)} %param.4) | copy-start | bytes 1769476
  1.1 6.9 %collective-permute-start = (f32[96,384]{1,0:T(8,128)S(1)}, f32[96,384]{1,0:T(8,128)S(1)}, u32[]{:S(2)}, u32[]{:S(2)}) collective-permute-start(f32[96,384]{1,0:T(8,128)S(1)} %get-tuple-element.32), channel_id=1, source_target_pairs={{0,2},{2,0},{1,3},{3,1},{4,6},{6,4},{5,7},{7,5},{8,10},{10,8},{9,1... | collective-permute-start | bytes 442376 | tf_op jit(solution)/shard_map/ppermute | solution.py:417
  4.1 18.4 %collective-permute-start.2 = (f32[192,384]{1,0:T(8,128)S(1)}, f32[192,384]{1,0:T(8,128)S(1)}, u32[]{:S(2)}, u32[]{:S(2)}) collective-permute-start(f32[192,384]{1,0:T(8,128)S(1)} %get-tuple-element.29), channel_id=1, source_target_pairs={{8,4},{12,8},{9,5},{13,9},{10,6},{14,10},{11,7},{15,11},{24,20},{2... | collective-permute-start | bytes 884744 | tf_op jit(solution)/shard_map/ppermute | solution.py:440
  8.0 14.5 %collective-permute-start.1 = (f32[96,384]{1,0:T(8,128)S(1)}, f32[96,384]{1,0:T(8,128)S(1)}, u32[]{:S(2)}, u32[]{:S(2)}) collective-permute-start(f32[96,384]{1,0:T(8,128)S(1)} %get-tuple-element.17), channel_id=1, source_target_pairs={{0,2},{2,0},{1,3},{3,1},{4,6},{6,4},{5,7},{7,5},{8,10},{10,8},{9,1... | collective-permute-start | bytes 442376 | tf_op jit(solution)/shard_map/ppermute | solution.py:417
  22.6 0.7 copy-start
  27.4 8.9 %collective-permute-start.3 = (f32[200,384]{1,0:T(8,128)S(1)}, f32[200,384]{1,0:T(8,128)S(1)}, u32[]{:S(2)}, u32[]{:S(2)}) collective-permute-start(f32[200,384]{1,0:T(8,128)S(1)} %get-tuple-element.18.own_v), channel_id=1, source_target_pairs={{0,4},{12,8},{1,5},{13,9},{2,6},{14,10},{3,7},{15,11},{16,20},{28,... | collective-permute-start | bytes 921608 | tf_op jit(solution)/shard_map/ppermute | solution.py:464
  50.7 0.7 collective-permute-start.4
  79.5 13.8 %collective-permute-start.5 = (f32[16,384]{1,0:T(8,128)S(1)}, f32[16,384]{1,0:T(8,128)S(1)}, u32[]{:S(2)}, u32[]{:S(2)}) collective-permute-start(f32[16,384]{1,0:T(8,128)S(1)} %concatenate.19), channel_id=1, source_target_pairs={{4,0},{8,12},{5,1},{9,13},{6,2},{10,14},{7,3},{11,15},{20,16},{24,... | collective-permute-start | bytes 73736 | tf_op jit(solution)/shard_map/ppermute | solution.py:488
where the time goes:
time: 94.9 us; the launch traced here: 94.7 us
  Pallas kernels  60.8 us (64%)
  waiting for transfers between devices  20.9 us (22%)
  starting transfers between devices  11 us (12%)
  other arithmetic  1.16 us (1%)
    pallas_call x6, Pallas kernels, call(): pl.pallas_call(kernel, out_shape=[jax.ShapeDtypeStruct(shape, jnp.float32...  60.8 us
    ppermute x1, waiting for transfers between devices, local(): lax.ppermute(jnp.concatenate([middle, value_u]), 'slab', [(b, a) for a, b...  12.5 us
    ppermute x1, waiting for transfers between devices, local(): first_v = lax.ppermute(new_v, 'slab', pairs)  5.36 us
    ppermute x2, starting transfers between devices, gather_columns(): lax.ppermute(shard, 'orb', [(i, i ^ distance) for i in range(size)])  4.84 us
    ppermute x1, starting transfers between devices, local(): first_v = lax.ppermute(new_v, 'slab', pairs)  3.5 us
    ppermute x2, waiting for transfers between devices, gather_columns(): lax.ppermute(shard, 'orb', [(i, i ^ distance) for i in range(size)])  3.1 us
  transfers between devices with their start and end apart: 6, of which 3 were waited for; matrix products, arithmetic and copies ran while one was open for 0% of the time, Pallas kernels for 13%

commit v1 on v0

--- a/solution.py
+++ b/solution.py
@@ -159,60 +159,69 @@
     return jnp.broadcast_to(rows[:, at : at + 1], (TALL, LANES))
 
 
+def pick(rows, at):
+    return jnp.broadcast_to(rows[at : at + 1], (TALL, LANES))
+
+
+def total(terms):
+    while len(terms) > 1:
+        terms = [sum(terms[i : i + 2][1:], terms[i]) for i in range(0, len(terms), 2)]
+    return terms[0]
+
+
+def spread_columns(part, step, count):
+    return [(spread_lane(part, step + at), spread_lane(part, step + at + HALF)) for at in range(count)]
+
+
+def invert_home(panel, spun, work, row_id):
+    work = [tuple(jnp.where(row_id >= 0, half, 0.0) for half in value) for value in work]
+    diagonal = pick(work[0][0], 0)
+    for p in range(TALL):
+        here = row_id == p
+        real, imag = work[p]
+        factor = 1.0 / diagonal
+        across = {j: (pick(real, j), pick(imag, j)) for j in range(p + 1, TALL)}
+        if p + 1 < TALL:
+            diagonal = pick(work[p + 1][0], p + 1) - squared(across[p + 1]) * factor
+        real = jnp.where(here, real - 1.0, real)
+        imag = jnp.where(here, 0.0, imag)
+        for j in range(p + 1, TALL):
+            value = (across[j][0] * factor, across[j][1] * -factor)
+            work[j] = minus(work[j], product((real, imag), value))
+        row, turn = pick(panel, p) * factor, pick(spun, p) * factor
+        panel = panel - (real * row + imag * turn)
+        spun = spun - (real * turn - imag * row)
+    return panel, spun
+
+
 def invert_group(rows, first, sign, lane, row_id):
-    parts = [rows[start : start + TALL] for start in range(0, GROUP, TALL)]
-    for offset in range(0, GROUP, 4):
-        step = first + offset
-        home, inner = divmod(offset, TALL)
-        columns = [
-            [(spread_lane(part, step + at), spread_lane(part, step + at + HALF)) for at in range(4)]
-            for part in parts
-        ]
-        inverse = invert_four(
-            [
-                [
-                    tuple(spread_row(value, inner + i) for value in columns[home][j])
-                    if j >= i
-                    else None
-                    for j in range(4)
-                ]
-                for i in range(4)
-            ]
-        )
-        inside = (lane % HALF >= step) & (lane % HALF < step + 4)
-        cleared = jnp.where(inside, 0.0, parts[home])
-        turned = pltpu.roll(cleared, HALF, 1) * sign
-        plain, spun = [], []
-        for at in range(4):
-            plain.append(spread_row(cleared, inner + at) + jnp.where(lane == step + at, 1.0, 0.0))
-            spun.append(
-                spread_row(turned, inner + at) + jnp.where(lane == step + at + HALF, 1.0, 0.0)
-            )
-        new_rows, new_spins = [], []
-        for i in range(4):
-            new = spin = None
-            for j in range(4):
-                real, imag = inverse[i][j]
-                if i == j:
-                    term, turn = real * plain[j], real * spun[j]
-                else:
-                    term = real * plain[j] + imag * spun[j]
-                    turn = real * spun[j] - imag * plain[j]
-                new, spin = (term, turn) if new is None else (new + term, spin + turn)
-            new_rows.append(new)
-            new_spins.append(spin)
-        updated = []
-        for index, part in enumerate(parts):
-            fresh = jnp.where(inside, 0.0, part)
-            for i in range(4):
-                real, imag = columns[index][i]
-                fresh = fresh - (real * new_rows[i] + imag * new_spins[i])
-            if index == home:
-                for i in range(4):
-                    fresh = jnp.where(row_id == inner + i, new_rows[i], fresh)
-            updated.append(fresh)
-        parts = updated
-    return jnp.concatenate(parts, axis=0) if len(parts) > 1 else parts[0]
+    above, below = rows[:TALL], rows[TALL:]
+    inside = (lane % HALF >= first) & (lane % HALF < first + TALL)
+    after = (lane % HALF >= first + TALL) & (lane % HALF < first + GROUP)
+    home = spread_columns(above, first, TALL)
+    side = spread_columns(below, first, TALL)
+    panel = jnp.where(inside, 0.0, above)
+    spun = pltpu.roll(panel, HALF, 1) * sign + jnp.where(lane == first + row_id + HALF, 1.0, 0.0)
+    panel = panel + jnp.where(lane == first + row_id, 1.0, 0.0)
+    panel, spun = invert_home(panel, spun, home, row_id)
+    below = jnp.where(inside, 0.0, below) - total(
+        [side[p][0] * pick(panel, p) + side[p][1] * pick(spun, p) for p in range(TALL)]
+    )
+    step = first + TALL
+    home = spread_columns(below, step, TALL)
+    side = spread_columns(panel, step, TALL)
+    lower = jnp.where(after, 0.0, below)
+    turned = pltpu.roll(lower, HALF, 1) * sign + jnp.where(lane == step + row_id + HALF, 1.0, 0.0)
+    lower = lower + jnp.where(lane == step + row_id, 1.0, 0.0)
+    lower, turned = invert_home(lower, turned, home, row_id)
+    rows = [(pick(lower, p), pick(turned, p)) for p in range(TALL)]
+    panel = jnp.where(after, 0.0, panel) - total(
+        [side[p][0] * rows[p][0] + side[p][1] * rows[p][1] for p in range(TALL)]
+    )
+    spun = jnp.where(after, 0.0, spun) - total(
+        [side[p][0] * rows[p][1] - side[p][1] * rows[p][0] for p in range(TALL)]
+    )
+    return jnp.concatenate([panel, lower], axis=0), jnp.concatenate([spun, turned], axis=0)
 
 
 def spread_out(done, spun, first):
@@ -228,18 +237,24 @@
     sign = lane_sign((1, LANES))
     group = block[:GROUP]
     for first in range(0, HALF, GROUP):
-        done = invert_group(group, first, sign, lane, row_id)
-        spun = pltpu.roll(done, HALF, 1) * sign
+        done, spun = invert_group(group, first, sign, lane, row_id)
         inside = (lane % HALF >= first) & (lane % HALF < first + GROUP)
         following = first + GROUP
         if following < HALF:
-            old = block[following : following + GROUP]
-            group = jnp.where(inside, 0.0, old)
-            for at in range(GROUP):
-                group = group - (
-                    old[:, first + at : first + at + 1] * done[at : at + 1]
-                    + old[:, first + at + HALF : first + at + HALF + 1] * spun[at : at + 1]
+            parts = []
+            for start in range(following, following + GROUP, TALL):
+                old = block[start : start + TALL]
+                columns = spread_columns(old, first, GROUP)
+                parts.append(
+                    jnp.where(inside, 0.0, old)
+                    - total(
+                        [
+                            columns[at][0] * pick(done, at) + columns[at][1] * pick(spun, at)
+                            for at in range(GROUP)
+                        ]
+                    )
                 )
+            group = jnp.concatenate(parts, axis=0)
         rest = jnp.where(inside, 0.0, block) - dot(
             jnp.where(inside, block, 0.0), spread_out(done, spun, first)
         )

time: 94.9 us -> 74.5 us (0.79)
  Pallas kernels: 60.8 us -> 40.3 us
    pallas_call x6, Pallas kernels: 60.8 us -> 40.3 us  [call(): pl.pallas_call(kernel, out_shape=[jax.ShapeDtypeStruct(shape, jnp.float32...]
  transfers between devices with their start and end apart: 6 -> 6, of which waited for: 3 -> 3; matrix products, arithmetic and copies ran while one was open for 0% -> 0% of each run, Pallas kernels for 13% -> 10%
where the time goes in v1:
time: 74.5 us; the launch traced here: 74.2 us
  Pallas kernels  40.3 us (54%)
  waiting for transfers between devices  20.9 us (28%)
  starting transfers between devices  11 us (15%)
  other arithmetic  1.16 us (2%)
    pallas_call x6, Pallas kernels, call(): pl.pallas_call(kernel, out_shape=[jax.ShapeDtypeStruct(shape, jnp.float32...  40.3 us
    ppermute x1, waiting for transfers between devices, local(): lax.ppermute(jnp.concatenate([middle, value_u]), 'slab', [(b, a) for a, b...  12.5 us
    ppermute x1, waiting for transfers between devices, local(): first_v = lax.ppermute(new_v, 'slab', pairs)  5.36 us
    ppermute x2, starting transfers between devices, gather_columns(): lax.ppermute(shard, 'orb', [(i, i ^ distance) for i in range(size)])  4.84 us
    ppermute x1, starting transfers between devices, local(): first_v = lax.ppermute(new_v, 'slab', pairs)  3.5 us
    ppermute x2, waiting for transfers between devices, gather_columns(): lax.ppermute(shard, 'orb', [(i, i ^ distance) for i in range(size)])  3.1 us
  transfers between devices with their start and end apart: 6, of which 3 were waited for; matrix products, arithmetic and copies ran while one was open for 0% of the time, Pallas kernels for 10%

profile of v1, /device:TPU:0, one launch (start us, length us, event | category | flops | bytes accessed | tf_op | source)
XLA Modules:
  0.0 74.2 jit_solution(6389820657743588510)
XLA Ops:
  0.0 0.0 copy-start.1
  0.0 1.1 %select_bitcast_fusion = (f32[96,384]{1,0:T(8,128)S(1)}, f32[96,384]{1,0:T(8,128)S(1)}) fusion(f32[2,96,384]{2,1,0:T(8,128)} %param.3, pred[]{:T(512)S(6)} %lt.15), kind=kLoop, calls=%fused_computation.5 | loop fusion | flops 73728 | bytes 589825 | tf_op jit(solution)/shard_map/jit(_where)/select_n | solution.py:457
  1.1 3.0 %collective-permute-start = (f32[96,384]{1,0:T(8,128)S(1)}, f32[96,384]{1,0:T(8,128)S(1)}, u32[]{:S(2)}, u32[]{:S(2)}) collective-permute-start(f32[96,384]{1,0:T(8,128)S(1)} %get-tuple-element.32), channel_id=1, source_target_pairs={{0,2},{2,0},{1,3},{3,1},{4,6},{6,4},{5,7},{7,5},{8,10},{10,8},{9,1... | collective-permute-start | bytes 442376 | tf_op jit(solution)/shard_map/ppermute | solution.py:432
  4.1 0.0 copy-done.1
  4.1 0.7 collective-permute-start.2
  4.9 3.1 %collective-permute-done = f32[96,384]{1,0:T(8,128)S(1)} collective-permute-done((f32[96,384]{1,0:T(8,128)S(1)}, f32[96,384]{1,0:T(8,128)S(1)}, u32[]{:S(2)}, u32[]{:S(2)}) %collective-permute-start) | collective-permute-done | bytes 147488 | tf_op jit(solution)/shard_map/ppermute | solution.py:432
  8.0 1.8 %collective-permute-start.1 = (f32[96,384]{1,0:T(8,128)S(1)}, f32[96,384]{1,0:T(8,128)S(1)}, u32[]{:S(2)}, u32[]{:S(2)}) collective-permute-start(f32[96,384]{1,0:T(8,128)S(1)} %get-tuple-element.17), channel_id=1, source_target_pairs={{0,2},{2,0},{1,3},{3,1},{4,6},{6,4},{5,7},{7,5},{8,10},{10,8},{9,1... | collective-permute-start | bytes 442376 | tf_op jit(solution)/shard_map/ppermute | solution.py:432
  9.8 7.6 %shard_map.37.inverse = f32[192,384]{1,0:T(8,128)S(1)} custom-call(f32[192,384]{1,0:T(8,128)S(1)} %maximum_select_fusion.block), custom_call_target="tpu_custom_call" | custom-call | flops 1811939328 | bytes 28311552 | tf_op jit(solution)/shard_map/pallas_call | solution.py:416
  17.4 0.0 collective-permute-done.1
  17.4 0.0 copy-start
  17.5 0.0 collective-permute-done.2
  17.5 0.7 copy-done
  18.2 4.1 %shard_map.38 = (f32[200,384]{1,0:T(8,128)S(1)}, f32[200,384]{1,0:T(8,128)S(1)}, f32[192,384]{1,0:T(8,128)S(1)}, f32[192,384]{1,0:T(8,128)S(1)}, f32[8,384]{1,0:T(8,128)S(1)}, /*index=5*/f32[192,384]{1,0:T(8,128)S(1)}) custom-call(f32[192,384]{1,0:T(8,128)S(1)} %shard_map.37.inverse, f32[192,384]{1,0:T(8,128)S(1)} %maximum_select_fusion.1.boundary, ...), custom_call_target="tpu_custom_call" | custom-call | tf_op jit(solution)/shard_map/pallas_call | solution.py:416
  22.3 3.5 %collective-permute-start.3 = (f32[200,384]{1,0:T(8,128)S(1)}, f32[200,384]{1,0:T(8,128)S(1)}, u32[]{:S(2)}, u32[]{:S(2)}) collective-permute-start(f32[200,384]{1,0:T(8,128)S(1)} %get-tuple-element.18.own_v), channel_id=1, source_target_pairs={{0,4},{12,8},{1,5},{13,9},{2,6},{14,10},{3,7},{15,11},{16,20},{28,... | collective-permute-start | bytes 921608 | tf_op jit(solution)/shard_map/ppermute | solution.py:479
  25.8 5.4 %collective-permute-done.3.first_v = f32[200,384]{1,0:T(8,128)S(1)} collective-permute-done((f32[200,384]{1,0:T(8,128)S(1)}, f32[200,384]{1,0:T(8,128)S(1)}, u32[]{:S(2)}, u32[]{:S(2)}) %collective-permute-start.3) | collective-permute-done | bytes 307232 | tf_op jit(solution)/shard_map/ppermute | solution.py:479
  31.2 9.2 %shard_map.39 = (f32[200,384]{1,0:T(8,128)S(1)}, f32[192,384]{1,0:T(8,128)S(1)}, f32[8,384]{1,0:T(8,128)S(1)}) custom-call(f32[200,384]{1,0:T(8,128)S(1)} %get-tuple-element.18.own_v, f32[200,384]{1,0:T(8,128)S(1)} %get-tuple-element.19.own_u, f32[192,384]{1,0:T(8,128)S(1)} %get-tuple-element.20.own_cross, f32[200,384]{1,0:T(8,128)S(1)} %collective-permute-done.3.first_v), custom_call_target="tpu_custom_call" | custom-call | tf_op jit(solution)/shard_map/pallas_call | solution.py:416
  40.4 0.7 collective-permute-start.4
  41.1 0.0 collective-permute-done.4.other
  41.1 17.4 %shard_map.40.value_v = f32[8,384]{1,0:T(8,128)S(1)} custom-call(f32[200,384]{1,0:T(8,128)S(1)} %get-tuple-element.21.own, f32[200,384]{1,0:T(8,128)S(1)} %collective-permute-done.4.other, f32[192,384]{1,0:T(8,128)S(1)} %get-tuple-element.27.coupling), custom_call_target="tpu_custom_call" | custom-call | tf_op jit(solution)/shard_map/pallas_call | solution.py:416
  58.6 0.5 shard_map.41
  59.0 1.3 %collective-permute-start.5 = (f32[16,384]{1,0:T(8,128)S(1)}, f32[16,384]{1,0:T(8,128)S(1)}, u32[]{:S(2)}, u32[]{:S(2)}) collective-permute-start(f32[16,384]{1,0:T(8,128)S(1)} %concatenate.19), channel_id=1, source_target_pairs={{4,0},{8,12},{5,1},{9,13},{6,2},{10,14},{7,3},{11,15},{20,16},{24,... | collective-permute-start | bytes 73736 | tf_op jit(solution)/shard_map/ppermute | solution.py:503
  60.4 12.5 %collective-permute-done.5 = f32[16,384]{1,0:T(8,128)S(1)} collective-permute-done((f32[16,384]{1,0:T(8,128)S(1)}, f32[16,384]{1,0:T(8,128)S(1)}, u32[]{:S(2)}, u32[]{:S(2)}) %collective-permute-start.5) | collective-permute-done | bytes 24608 | tf_op jit(solution)/shard_map/ppermute | solution.py:503
  72.8 1.4 %shard_map.42 = f32[2,8,384]{2,1,0:T(8,128)} custom-call(f32[8,384]{1,0:T(8,128)S(1)} %get-tuple-element.34.value_v, f32[8,384]{1,0:T(8,128)S(1)} %get-tuple-element.33.value_u, f32[192,384]{1,0:T(8,128)S(1)} %get-tuple-element.24.kept_v, f32[8,384]{1,0:T(8,128)S(1)} %get-tuple-element.25.kept_b, f32[192,384]{1,0:T(8,128)S(1)} %get-tuple-element.26.kept_u), custom_call_target="tpu_custom_call" | custom-call | tf_op jit(solution)/shard_map/pallas_call | solution.py:416
  (6 shorter events, 0.1 us)
Async XLA Ops:
  0.0 4.1 %copy-start.1 = (f32[2,192,384]{2,1,0:T(8,128)S(1)}, f32[2,192,384]{2,1,0:T(8,128)}, u32[]{:S(2)}) copy-start(f32[2,192,384]{2,1,0:T(8,128)} %param.4) | copy-start | bytes 1769476
  1.1 6.9 %collective-permute-start = (f32[96,384]{1,0:T(8,128)S(1)}, f32[96,384]{1,0:T(8,128)S(1)}, u32[]{:S(2)}, u32[]{:S(2)}) collective-permute-start(f32[96,384]{1,0:T(8,128)S(1)} %get-tuple-element.32), channel_id=1, source_target_pairs={{0,2},{2,0},{1,3},{3,1},{4,6},{6,4},{5,7},{7,5},{8,10},{10,8},{9,1... | collective-permute-start | bytes 442376 | tf_op jit(solution)/shard_map/ppermute | solution.py:432
  4.1 13.3 %collective-permute-start.2 = (f32[192,384]{1,0:T(8,128)S(1)}, f32[192,384]{1,0:T(8,128)S(1)}, u32[]{:S(2)}, u32[]{:S(2)}) collective-permute-start(f32[192,384]{1,0:T(8,128)S(1)} %get-tuple-element.29), channel_id=1, source_target_pairs={{8,4},{12,8},{9,5},{13,9},{10,6},{14,10},{11,7},{15,11},{24,20},{2... | collective-permute-start | bytes 884744 | tf_op jit(solution)/shard_map/ppermute | solution.py:455
  8.0 9.4 %collective-permute-start.1 = (f32[96,384]{1,0:T(8,128)S(1)}, f32[96,384]{1,0:T(8,128)S(1)}, u32[]{:S(2)}, u32[]{:S(2)}) collective-permute-start(f32[96,384]{1,0:T(8,128)S(1)} %get-tuple-element.17), channel_id=1, source_target_pairs={{0,2},{2,0},{1,3},{3,1},{4,6},{6,4},{5,7},{7,5},{8,10},{10,8},{9,1... | collective-permute-start | bytes 442376 | tf_op jit(solution)/shard_map/ppermute | solution.py:432
  17.4 0.7 copy-start
  22.3 8.9 %collective-permute-start.3 = (f32[200,384]{1,0:T(8,128)S(1)}, f32[200,384]{1,0:T(8,128)S(1)}, u32[]{:S(2)}, u32[]{:S(2)}) collective-permute-start(f32[200,384]{1,0:T(8,128)S(1)} %get-tuple-element.18.own_v), channel_id=1, source_target_pairs={{0,4},{12,8},{1,5},{13,9},{2,6},{14,10},{3,7},{15,11},{16,20},{28,... | collective-permute-start | bytes 921608 | tf_op jit(solution)/shard_map/ppermute | solution.py:479
  40.4 0.7 collective-permute-start.4
  59.0 13.8 %collective-permute-start.5 = (f32[16,384]{1,0:T(8,128)S(1)}, f32[16,384]{1,0:T(8,128)S(1)}, u32[]{:S(2)}, u32[]{:S(2)}) collective-permute-start(f32[16,384]{1,0:T(8,128)S(1)} %concatenate.19), channel_id=1, source_target_pairs={{4,0},{8,12},{5,1},{9,13},{6,2},{10,14},{7,3},{11,15},{20,16},{24,... | collective-permute-start | bytes 73736 | tf_op jit(solution)/shard_map/ppermute | solution.py:503

commit v2 on v1

--- a/solution.py
+++ b/solution.py
@@ -231,11 +231,13 @@
     return jnp.concatenate(before + [done] + after + before + [spun] + after, axis=0)
 
 
-def invert_small(block):
+def invert_small(block, fillers=()):
     lane = lax.broadcasted_iota(jnp.int32, (1, LANES), 1)
     row_id = lax.broadcasted_iota(jnp.int32, (TALL, 1), 0)
     sign = lane_sign((1, LANES))
     group = block[:GROUP]
+    fillers = list(fillers)
+    slots = HALF // GROUP
     for first in range(0, HALF, GROUP):
         done, spun = invert_group(group, first, sign, lane, row_id)
         inside = (lane % HALF >= first) & (lane % HALF < first + GROUP)
@@ -261,166 +263,317 @@
         above = [rest[:first]] if first else []
         below = [rest[following:]] if following < HALF else []
         block = jnp.concatenate(above + [done] + below, axis=0)
+        share = -(-len(fillers) // slots)
+        for filler in fillers[:share]:
+            filler()
+        fillers, slots = fillers[share:], slots - 1
     return block
 
 
-def invert(ref):
-    order = ref.shape[0]
-
-    def step(k, carry):
-        rows = pl.ds(pl.multiple_of(k * HALF, HALF), HALF)
-        lanes = pl.ds(pl.multiple_of(k * LANES, LANES), LANES)
-        small = invert_small(ref[rows, lanes])
-        panel = ref[rows, :]
-        ref[rows, :] = dot(small, jnp.concatenate([panel, times_i(panel)], axis=0))
-        ref[rows, lanes] = small
-        fresh = ref[rows, :]
-        column = ref[:, lanes]
-        ref[:, lanes] = jnp.zeros((order, LANES), jnp.float32)
-        ref[...] = ref[...] - dot(column, jnp.concatenate([fresh, times_i(fresh)], axis=0))
-        ref[rows, :] = fresh
-        return carry
-
-    lax.fori_loop(0, order // HALF, step, 0)
-
-
-def eliminate(pivot_ref, to_pivot_v, to_pivot_u, block_v, block_u, load_i, load_v, load_u):
-    invert(pivot_ref)
-    return apply_pivot(
-        pivot_ref, to_pivot_v, to_pivot_u, block_v, block_u, load_i, load_v, load_u
-    )
-
-
-def apply_pivot(pivot_ref, to_pivot_v, to_pivot_u, block_v, block_u, load_i, load_v, load_u):
-    order, rhs = block_v.shape[0], load_i.shape[0]
-    inverse = embed(pivot_ref[...])
-    stacked = [compact(to_pivot_v), load_i]
-    if to_pivot_u is not None:
-        stacked.append(compact(to_pivot_u))
-    through = dot(jnp.concatenate(stacked, axis=0), inverse)
-    toward_v = dot_flipped(through[: order + rhs], to_pivot_v)
-    new_v = jnp.concatenate([block_v, load_v], axis=0) - toward_v
-    kept = (through[:order], through[order : order + rhs])
-    if to_pivot_u is None:
-        return new_v, kept
-    toward_u = dot_flipped(through, to_pivot_u)
-    new_u = jnp.concatenate([block_u, load_u], axis=0) - jnp.concatenate(
-        [toward_u[order + rhs :], toward_u[order : order + rhs]], axis=0
-    )
-    return new_v, new_u, -toward_u[:order], kept + (through[order + rhs :],)
+def doubled(rows):
+    return jnp.concatenate([rows, times_i(rows)], axis=0)
+
+
+def chunk(rows, at):
+    return rows[:, at * LANES : (at + 1) * LANES]
+
+
+def eliminate(pivot, tail, toward):
+    count = pivot.shape[0] // HALF
+    blocks = [
+        [chunk(pivot[i * HALF : (i + 1) * HALF], k) for k in range(count)] for i in range(count)
+    ]
+    tails = [chunk(tail, k) for k in range(count)] if tail is not None else None
+    scaled = [None] * count
+    lower = {}
+    sums = [None] * len(toward)
+    pending = []
+
+    def bulk(k, inverse, across):
+        def rows_below(i):
+            def run():
+                lower[i, k] = dot(blocks[i][k], inverse)
+                change = dot(lower[i, k], across)
+                for c in range(k + 1, count):
+                    blocks[i][c] = blocks[i][c] - chunk(change, c - k - 1)
+
+            return run
+
+        def scale():
+            scaled[k] = dot(tails[k], inverse)
+
+        def shift():
+            change = dot(scaled[k], across)
+            for c in range(k + 1, count):
+                tails[c] = tails[c] - chunk(change, c - k - 1)
+
+        def gather(at):
+            def run():
+                (first, last), (low, high) = toward[at]
+                term = dot_flipped(scaled[k][first:last], embed(tails[k][low:high]))
+                sums[at] = term if sums[at] is None else sums[at] + term
+
+            return run
+
+        work = [rows_below(i) for i in range(k + 2, count)] + [scale]
+        if k + 1 < count:
+            work.append(shift)
+        return work + [gather(at) for at in range(len(toward))]
+
+    for k in range(count):
+        inverse = doubled(invert_small(blocks[k][k], pending))
+        across = None
+        if k + 1 < count:
+            across = doubled(jnp.concatenate(blocks[k][k + 1 :], axis=1))
+            lower[k + 1, k] = dot(blocks[k + 1][k], inverse)
+            change = dot(lower[k + 1, k], across)
+            for c in range(k + 1, count):
+                blocks[k + 1][c] = blocks[k + 1][c] - chunk(change, c - k - 1)
+        pending = bulk(k, inverse, across)
+    for work in pending:
+        work()
+    stacked = [lower[i, k] for k in range(count) for i in range(k + 1, count)]
+    return jnp.concatenate(scaled, axis=1), jnp.concatenate(stacked, axis=0), sums
+
+
+def resolve(rows, lower):
+    count = rows.shape[1] // LANES
+    places = [(i, k) for k in range(count) for i in range(k + 1, count)]
+    found = [chunk(rows, k) for k in range(count)]
+    for i in range(count - 1, 0, -1):
+        for k in range(i):
+            at = places.index((i, k)) * HALF
+            found[k] = found[k] - dot(found[i], doubled(lower[at : at + HALF]))
+    return jnp.concatenate(found, axis=1)
 
 
 def flip_where(flip, ref, embedded):
     @pl.when(flip)
     def _():
-        ref[...] = embedded.T
+        ref[...] = compact(embedded.T)
 
     @pl.when(jnp.logical_not(flip))
     def _():
-        ref[...] = embedded
+        ref[...] = compact(embedded)
 
 
 def is_left():
     return lax.axis_index("slab") < lax.axis_size("slab") // 2
 
 
-def invert_kernel(block, inverse):
-    inverse[...] = interleave(block[...])
-    invert(inverse)
-
-
 def interior_kernel(
-    inverse, boundary, inner, outer, loads,
-    new_v, new_u, cross, kept_v, kept_b, kept_u, to_v, to_u,
+    interior, inner, outer, loads, sum_v, new_u, cross, kept_v, kept_b, kept_u, lower, to_v, to_u
 ):
     left = is_left()
     at_interior = jnp.where(left, 0, 1)
     flip_where(left, to_v, embed(interleave(inner[...])))
     flip_where(jnp.logical_not(left), to_u, embed(interleave(outer[...])))
     load_i = interleave(loads[at_interior])
+    order, rhs = to_v.shape[0], load_i.shape[0]
+    tail = jnp.concatenate([to_v[...], load_i, to_u[...]], axis=0)
+    both, end = order + rhs, 2 * order + rhs
+    scaled, lower[...], sums = eliminate(
+        interleave(interior[...]), tail, [((0, both), (0, order)), ((0, end), (both, end))]
+    )
+    sum_v[...] = sums[0]
+    new_u[...] = -jnp.concatenate([sums[1][both:], sums[1][order:both]], axis=0)
+    cross[...] = -sums[1][:order]
+    kept_v[...], kept_b[...], kept_u[...] = scaled[:order], scaled[order:both], scaled[both:]
+
+
+def boundary_kernel(boundary, loads, sum_v, new_v):
+    at_interior = jnp.where(is_left(), 0, 1)
     load_v = interleave(loads[1 - at_interior])
-    block_v = interleave(boundary[...])
-    zero = jnp.zeros_like(block_v)
-    new_v[...], new_u[...], cross[...], kept = apply_pivot(
-        inverse, to_v[...], to_u[...], block_v, zero, load_i, load_v, jnp.zeros_like(load_v)
-    )
-    kept_v[...], kept_b[...], kept_u[...] = kept
-
-
-def level_kernel(own_v, own_u, own_cross, first_v, new_v, kept_v, kept_b, pivot):
-    order = pivot.shape[0]
+    order = boundary.shape[0]
+    new_v[:order] = interleave(boundary[...]) - sum_v[:order]
+    new_v[order:] = load_v - sum_v[order:]
+
+
+def level_kernel(own_v, own_u, own_cross, first_v, new_v, kept_v, kept_b, lower):
+    order = own_cross.shape[0]
     joined = first_v[...] + own_u[...]
-    pivot[...] = joined[:order]
-    new_v[...], kept = eliminate(
-        pivot, embed(own_cross[...]), None, own_v[:order], None, joined[order:], own_v[order:], None
-    )
-    kept_v[...], kept_b[...] = kept
+    tail = jnp.concatenate([own_cross[...], joined[order:]], axis=0)
+    scaled, lower[...], sums = eliminate(joined[:order], tail, [((0, tail.shape[0]), (0, order))])
+    new_v[...] = own_v[...] - sums[0]
+    kept_v[...], kept_b[...] = scaled[:order], scaled[order:]
 
 
 def wide_level_kernel(
     own_v, own_u, own_cross, first_v, first_u, first_cross,
-    new_v, new_u, cross, kept_v, kept_b, kept_u, pivot,
+    new_v, new_u, cross, kept_v, kept_b, kept_u, lower,
 ):
-    order = pivot.shape[0]
+    order = own_cross.shape[0]
     joined = first_v[...] + own_u[...]
-    pivot[...] = joined[:order]
-    new_v[...], new_u[...], cross[...], kept = eliminate(
-        pivot,
-        embed(own_cross[...]),
-        embed(first_cross[...]).T,
-        own_v[:order],
-        first_u[:order],
-        joined[order:],
-        own_v[order:],
-        first_u[order:],
-    )
-    kept_v[...], kept_b[...], kept_u[...] = kept
-
-
-def center_kernel(own, other, coupling, value, pivot, to_other):
-    order = pivot.shape[0]
-    flip_where(jnp.logical_not(is_left()), to_other, embed(interleave(coupling[...])))
-    pivot[...] = other[:order]
-    reduced, _ = eliminate(
-        pivot, to_other[...], None, own[:order], None, other[order:], own[order:], None
-    )
-    pivot[...] = reduced[:order]
-    invert(pivot)
-    value[...] = dot(reduced[order:], embed(pivot[...]))
-
-
-def back_kernel(value_v, value_u, kept_v, kept_b, kept_u, middle):
-    middle[...] = (
+    tail = jnp.concatenate(
+        [own_cross[...], joined[order:], compact(embed(first_cross[...]).T)], axis=0
+    )
+    both, end = joined.shape[0], tail.shape[0]
+    scaled, lower[...], sums = eliminate(
+        joined[:order], tail, [((0, both), (0, order)), ((0, end), (both, end))]
+    )
+    new_v[...] = own_v[...] - sums[0]
+    new_u[...] = first_u[...] - jnp.concatenate([sums[1][both:], sums[1][order:both]], axis=0)
+    cross[...] = -sums[1][:order]
+    kept_v[...], kept_b[...], kept_u[...] = scaled[:order], scaled[order:both], scaled[both:]
+
+
+PIECES = 2
+
+
+def greet(partners):
+    barrier = pltpu.get_barrier_semaphore()
+    for partner in partners:
+        pl.semaphore_signal(barrier, inc=1, device_id=partner, device_id_type=pl.DeviceIdType.MESH)
+    pl.semaphore_wait(barrier, len(partners))
+
+
+def siblings():
+    size = lax.axis_size("rhs")
+    return [{"rhs": lax.rem(lax.axis_index("rhs") + step, size)} for step in range(1, size)]
+
+
+def remote(source, target, send, receive, device):
+    return pltpu.make_async_remote_copy(
+        src_ref=source, dst_ref=target, send_sem=send, recv_sem=receive,
+        device_id=device, device_id_type=pl.DeviceIdType.MESH,
+    )
+
+
+class Relay:
+    def __init__(self, source, target, device, order, sems):
+        self.source, self.target, self.device, self.order = source, target, device, order
+        self.send, self.receive, self.pass_send, self.pass_receive = sems
+        self.cores = lax.axis_size("rhs")
+        self.piece = order // self.cores // PIECES
+
+    def rows(self, core, piece):
+        start = (core * PIECES + piece) * self.piece
+        return pl.ds(pl.multiple_of(start, 8), self.piece)
+
+    def copies(self):
+        core = lax.axis_index("rhs")
+        own = [
+            remote(
+                self.source.at[self.rows(core, piece)], self.target.at[self.rows(core, piece)],
+                self.send.at[piece], self.receive.at[piece], self.device,
+            )
+            for piece in range(PIECES)
+        ]
+        after = pl.ds(self.order, self.source.shape[0] - self.order)
+        own.append(
+            remote(
+                self.source.at[after], self.target.at[after],
+                self.send.at[PIECES], self.receive.at[PIECES], self.device,
+            )
+        )
+        return own
+
+    def passes(self, piece):
+        core = lax.axis_index("rhs")
+        rows = self.rows(core, piece)
+        return [
+            remote(
+                self.target.at[rows], self.target.at[rows],
+                self.pass_send.at[piece, step], self.pass_receive.at[piece, step], device,
+            )
+            for step, device in enumerate(siblings())
+        ]
+
+    def start(self):
+        for copy in self.copies():
+            copy.start()
+
+    def wait_sent(self):
+        for copy in self.copies():
+            copy.wait_send()
+
+    def wait_received(self):
+        arrived = self.copies()
+        for piece in range(PIECES):
+            arrived[piece].wait_recv()
+            for copy in self.passes(piece):
+                copy.start()
+        arrived[PIECES].wait_recv()
+        for piece in range(PIECES):
+            for copy in self.passes(piece):
+                copy.wait()
+
+
+def relay_semaphores():
+    passing = (PIECES, max(1, lax.axis_size("rhs") - 1))
+    return [
+        pltpu.SemaphoreType.DMA((PIECES + 1,)), pltpu.SemaphoreType.DMA((PIECES + 1,)),
+        pltpu.SemaphoreType.DMA(passing), pltpu.SemaphoreType.DMA(passing),
+    ]
+
+
+def center_kernel(own, coupling, value, other, to_other, *sems):
+    order = coupling.shape[0]
+    half = lax.axis_size("slab") // 2
+    slab = lax.axis_index("slab")
+    left = is_left()
+    middle = (slab == half - 1) | (slab == half)
+
+    @pl.when(middle)
+    def _():
+        partner = {"slab": jnp.where(left, half, half - 1)}
+        greet([partner] + siblings())
+        relay = Relay(own, other, partner, order, sems)
+        relay.start()
+        flip_where(jnp.logical_not(left), to_other, embed(interleave(coupling[...])))
+        relay.wait_received()
+        tail = jnp.concatenate([to_other[...], other[order:]], axis=0)
+        _, _, sums = eliminate(other[:order], tail, [((0, tail.shape[0]), (0, order))])
+        reduced = own[...] - sums[0]
+        scaled, lower, _ = eliminate(reduced[:order], reduced[order:], [])
+        value[...] = resolve(scaled, lower)
+        relay.wait_sent()
+
+    @pl.when(jnp.logical_not(middle))
+    def _():
+        value[...] = jnp.zeros(value.shape, jnp.float32)
+
+
+def back_kernel(value_v, value_u, kept_v, kept_b, kept_u, lower, middle):
+    found = (
         kept_b[...]
         - dot(value_v[...], embed(kept_v[...]))
         - dot(value_u[...], embed(kept_u[...]))
     )
-
-
-def narrow_back_kernel(value_v, kept_v, kept_b, middle):
-    middle[...] = kept_b[...] - dot(value_v[...], embed(kept_v[...]))
-
-
-def final_kernel(value_v, value_u, kept_v, kept_b, kept_u, result):
-    middle = (
+    middle[...] = resolve(found, lower[...])
+
+
+def narrow_back_kernel(value_v, kept_v, kept_b, lower, middle):
+    middle[...] = resolve(kept_b[...] - dot(value_v[...], embed(kept_v[...])), lower[...])
+
+
+def final_kernel(value_v, value_u, kept_v, kept_b, kept_u, lower, result):
+    found = (
         kept_b[...]
         - dot(value_v[...], embed(kept_v[...]))
         - dot(value_u[...], embed(kept_u[...]))
     )
     at_interior = jnp.where(is_left(), 0, 1)
-    result[at_interior] = separate(middle)
+    result[at_interior] = separate(resolve(found, lower[...]))
     result[1 - at_interior] = separate(value_v[...])
 
 
-def call(kernel, outs, scratch, *operands, flops=0):
+def call(kernel, outs, scratch, *operands, flops=0, collective_id=None):
     return pl.pallas_call(
         kernel,
         out_shape=[jax.ShapeDtypeStruct(shape, jnp.float32) for shape in outs],
-        scratch_shapes=[pltpu.VMEM(shape, jnp.float32) for shape in scratch],
+        scratch_shapes=[
+            pltpu.VMEM(shape, jnp.float32) if isinstance(shape, tuple) else shape
+            for shape in scratch
+        ],
         cost_estimate=pl.CostEstimate(flops=flops, bytes_accessed=flops // 64, transcendentals=0)
         if flops
         else None,
-        compiler_params=pltpu.CompilerParams(vmem_limit_bytes=48 * 1024 * 1024),
+        compiler_params=pltpu.CompilerParams(
+            vmem_limit_bytes=48 * 1024 * 1024,
+            collective_id=collective_id,
+            has_side_effects=collective_id is not None,
+        ),
     )(*operands)
 
 
@@ -459,15 +612,17 @@
     boundary = gather_columns(held)
     outer = jnp.where(left, jnp.where(slab > 0, couplings[0], 0.0), shifted)
     center = jnp.where(left, shifted, couplings[0])
-    square, tall, thin, full = (order, width), (order + rhs, width), (rhs, width), (width, width)
-
-    (inverse,) = call(invert_kernel, [square], [], interior, flops=64 * order * width * width)
-    new_v, new_u, cross, kept_v, kept_b, kept_u = call(
+    square, tall, thin = (order, width), (order + rhs, width), (rhs, width)
+    count = order // HALF
+    below = (count * (count - 1) // 2 * HALF, LANES)
+
+    sum_v, new_u, cross, kept_v, kept_b, kept_u, lower = call(
         interior_kernel,
-        [tall, tall, square, square, thin, square],
-        [full, full],
-        inverse, boundary, couplings[1], outer, sources,
-    )
+        [tall, tall, square, square, thin, square, below],
+        [square, square],
+        interior, couplings[1], outer, sources, flops=64 * order * width * width,
+    )
+    (new_v,) = call(boundary_kernel, [tall], [], boundary, sources, sum_v)
     levels = half.bit_length() - 1
     stored = []
     for level in range(levels):
@@ -478,25 +633,29 @@
         ]
         first_v = lax.ppermute(new_v, "slab", pairs)
         if level == levels - 1:
-            new_v, level_v, level_b = call(
-                level_kernel, [tall, square, thin], [square], new_v, new_u, cross, first_v
+            new_v, level_v, level_b, level_l = call(
+                level_kernel, [tall, square, thin, below], [], new_v, new_u, cross, first_v
             )
-            stored.append((distance, pairs, (level_v, level_b)))
+            stored.append((distance, pairs, (level_v, level_b, level_l)))
         else:
             first_u = lax.ppermute(new_u, "slab", pairs)
             first_cross = lax.ppermute(cross, "slab", pairs)
-            new_v, new_u, cross, level_v, level_b, level_u = call(
+            new_v, new_u, cross, level_v, level_b, level_u, level_l = call(
                 wide_level_kernel,
-                [tall, tall, square, square, thin, square],
-                [square],
+                [tall, tall, square, square, thin, square, below],
+                [],
                 new_v, new_u, cross, first_v, first_u, first_cross,
             )
-            stored.append((distance, pairs, (level_v, level_b, level_u)))
-    other = lax.ppermute(new_v, "slab", [(half - 1, half), (half, half - 1)])
-    (value_v,) = call(center_kernel, [thin], [square, full], new_v, other, center)
+            stored.append((distance, pairs, (level_v, level_b, level_u, level_l)))
+    (value_v,) = call(
+        center_kernel,
+        [thin],
+        [pltpu.VMEM(tall, jnp.float32), pltpu.VMEM(square, jnp.float32), *relay_semaphores()],
+        new_v, center, collective_id=1,
+    )
     value_u = jnp.zeros_like(value_v)
     for distance, pairs, kept in reversed(stored):
-        if len(kept) == 2:
+        if len(kept) == 3:
             (middle,) = call(narrow_back_kernel, [thin], [], value_v, *kept)
         else:
             (middle,) = call(back_kernel, [thin], [], value_v, value_u, *kept)
@@ -507,7 +666,7 @@
         value_v = jnp.where(is_first, sent[:rhs], value_v)
         value_u = jnp.where(is_first, sent[rhs:], middle)
     (result,) = call(
-        final_kernel, [sources.shape], [], value_v, value_u, kept_v, kept_b, kept_u
+        final_kernel, [sources.shape], [], value_v, value_u, kept_v, kept_b, kept_u, lower
     )
     return result
 

time: 74.5 us -> 70.4 us (0.945)
  Pallas kernels: 40.3 us -> 20.5 us
  waiting for transfers between devices: 20.9 us -> 35.1 us
  starting transfers between devices: 11 us -> 13.1 us
  other arithmetic: 1.16 us -> 0.12 us
    pallas_call x6, Pallas kernels: 40.3 us -> 20.5 us  [call(): pl.pallas_call(kernel, out_shape=[jax.ShapeDtypeStruct(shape, jnp.float32...]
    ppermute x1, waiting for transfers between devices: 12.5 us -> 25.8 us  [local(): lax.ppermute(jnp.concatenate([middle, value_u]), 'slab', [(b, a) for a, b...]
    ppermute x1, starting transfers between devices: 3.5 us -> 6.32 us  [local(): first_v = lax.ppermute(new_v, 'slab', pairs)]
    squeeze x1, local copies, waits for them, and re-layouts: 0.04 us -> 1.13 us  [local(): outer = jnp.where(left, jnp.where(slab > 0, couplings[0], 0.0), shifted)]
    select_n x1, other arithmetic: 1.06 us -> 0.02 us  [local(): held = jnp.where(left, diag_blocks[1], diag_blocks[0])]
    ppermute x2, waiting for transfers between devices: 3.1 us -> 3.85 us  [gather_columns(): lax.ppermute(shard, 'orb', [(i, i ^ distance) for i in range(size)])]
  transfers between devices with their start and end apart: 6 -> 5, of which waited for: 3 -> 3; matrix products, arithmetic and copies ran while one was open for 0% -> 0% of each run, Pallas kernels for 10% -> 14%
where the time goes in v2:
time: 70.4 us; the launch traced here: 70.2 us
  waiting for transfers between devices  35.1 us (50%)
  Pallas kernels  20.5 us (29%)
  starting transfers between devices  13.1 us (19%)
  local copies, waits for them, and re-layouts  1.16 us (2%)
    ppermute x1, waiting for transfers between devices, local(): lax.ppermute(jnp.concatenate([middle, value_u]), 'slab', [(b, a) for a, b...  25.8 us
    pallas_call x6, Pallas kernels, call(): pl.pallas_call(kernel, out_shape=[jax.ShapeDtypeStruct(shape, jnp.float32...  20.5 us
    ppermute x1, starting transfers between devices, local(): first_v = lax.ppermute(new_v, 'slab', pairs)  6.32 us
    ppermute x1, waiting for transfers between devices, local(): first_v = lax.ppermute(new_v, 'slab', pairs)  5.46 us
    ppermute x2, starting transfers between devices, gather_columns(): lax.ppermute(shard, 'orb', [(i, i ^ distance) for i in range(size)])  4.84 us
    ppermute x2, waiting for transfers between devices, gather_columns(): lax.ppermute(shard, 'orb', [(i, i ^ distance) for i in range(size)])  3.85 us
  transfers between devices with their start and end apart: 5, of which 3 were waited for; matrix products, arithmetic and copies ran while one was open for 0% of the time, Pallas kernels for 14%

profile of v2, /device:TPU:0, one launch (start us, length us, event | category | flops | bytes accessed | tf_op | source)
XLA Modules:
  0.0 70.2 jit_solution(10968297138340321816)
XLA Ops:
  0.0 0.0 copy-start.2
  0.0 1.1 %slice_bitcast_fusion = (f32[192,384]{1,0:T(8,128)S(1)}, f32[192,384]{1,0:T(8,128)S(1)}) fusion(f32[2,192,384]{2,1,0:T(8,128)} %param.4), kind=kLoop, calls=%fused_computation.3 | loop fusion | bytes 1179648 | tf_op jit(solution)/shard_map/squeeze | solution.py:613
  1.1 0.7 collective-permute-start.2
  1.8 0.0 copy-done.2
  1.8 0.0 copy-start.1
  1.9 3.0 %collective-permute-start = (f32[96,384]{1,0:T(8,128)S(1)}, f32[96,384]{1,0:T(8,128)S(1)}, u32[]{:S(2)}, u32[]{:S(2)}) collective-permute-start(f32[96,384]{1,0:T(8,128)S(1)} %get-tuple-element.36), channel_id=1, source_target_pairs={{0,2},{2,0},{1,3},{3,1},{4,6},{6,4},{5,7},{7,5},{8,10},{10,8},{9,1... | collective-permute-start | bytes 442376 | tf_op jit(solution)/shard_map/ppermute | solution.py:585
  4.9 3.8 %collective-permute-done = f32[96,384]{1,0:T(8,128)S(1)} collective-permute-done((f32[96,384]{1,0:T(8,128)S(1)}, f32[96,384]{1,0:T(8,128)S(1)}, u32[]{:S(2)}, u32[]{:S(2)}) %collective-permute-start) | collective-permute-done | bytes 147488 | tf_op jit(solution)/shard_map/ppermute | solution.py:585
  8.8 0.0 copy-start
  8.8 1.8 %collective-permute-start.1 = (f32[96,384]{1,0:T(8,128)S(1)}, f32[96,384]{1,0:T(8,128)S(1)}, u32[]{:S(2)}, u32[]{:S(2)}) collective-permute-start(f32[96,384]{1,0:T(8,128)S(1)} %get-tuple-element.18), channel_id=1, source_target_pairs={{0,2},{2,0},{1,3},{3,1},{4,6},{6,4},{5,7},{7,5},{8,10},{10,8},{9,1... | collective-permute-start | bytes 442376 | tf_op jit(solution)/shard_map/ppermute | solution.py:585
  10.6 0.0 collective-permute-done.2
  10.6 0.0 copy-done.1
  10.7 0.0 copy-done
  10.7 10.2 %shard_map.37 = (f32[200,384]{1,0:T(8,128)S(1)}, f32[200,384]{1,0:T(8,128)S(1)}, f32[192,384]{1,0:T(8,128)S(1)}, f32[192,384]{1,0:T(8,128)S(1)}, f32[8,384]{1,0:...) custom-call(f32[192,384]{1,0:T(8,128)S(1)} %maximum_select_fusion.interior, ...), custom_call_target="tpu_custom_call" | custom-call | flops 1811939328 | bytes 28311552 | tf_op jit(solution)/shard_map/pallas_call | solution.py:562
  20.9 0.0 collective-permute-done.1
  20.9 0.1 shard_map.38.own_v
  21.0 6.3 %collective-permute-start.3 = (f32[200,384]{1,0:T(8,128)S(1)}, f32[200,384]{1,0:T(8,128)S(1)}, u32[]{:S(2)}, u32[]{:S(2)}) collective-permute-start(f32[200,384]{1,0:T(8,128)S(1)} %shard_map.38.own_v), channel_id=1, source_target_pairs={{0,4},{12,8},{1,5},{13,9},{2,6},{14,10},{3,7},{15,11},{16,20},{28,... | collective-permute-start | bytes 921608 | tf_op jit(solution)/shard_map/ppermute | solution.py:634
  27.4 5.5 %collective-permute-done.3.first_v = f32[200,384]{1,0:T(8,128)S(1)} collective-permute-done((f32[200,384]{1,0:T(8,128)S(1)}, f32[200,384]{1,0:T(8,128)S(1)}, u32[]{:S(2)}, u32[]{:S(2)}) %collective-permute-start.3) | collective-permute-done | bytes 307232 | tf_op jit(solution)/shard_map/ppermute | solution.py:634
  32.8 7.6 %shard_map.39 = (f32[200,384]{1,0:T(8,128)S(1)}, f32[192,384]{1,0:T(8,128)S(1)}, f32[8,384]{1,0:T(8,128)S(1)}, f32[192,128]{1,0:T(8,128)S(1)}) custom-call(f32[200,384]{1,0:T(8,128)S(1)} %shard_map.38.own_v, f32[200,384]{1,0:T(8,128)S(1)} %get-tuple-element.21.own_u, f32[192,384]{1,0:T(8,128)S(1)} %get-tuple-element.22.own_cross, ...), custom_call_target="tpu_custom_call" | custom-call | tf_op jit(solution)/shard_map/pallas_call | solution.py:562
  40.4 0.1 shard_map.40.value_v
  40.5 0.8 %shard_map.41 = f32[8,384]{1,0:T(8,128)S(1)} custom-call(f32[8,384]{1,0:T(8,128)S(1)} %shard_map.40.value_v, f32[192,384]{1,0:T(8,128)S(1)} %get-tuple-element.24.kept_v, f32[8,384]{1,0:T(8,128)S(1)} %get-tuple-element.25.kept_b, f32[192,128]{1,0:T(8,128)S(1)} %get-tuple-element.26.lower), custom_call_target="tpu_custom_call" | custom-call | tf_op jit(solution)/shard_map/pallas_call | solution.py:562
  41.4 1.3 %collective-permute-start.4 = (f32[16,384]{1,0:T(8,128)S(1)}, f32[16,384]{1,0:T(8,128)S(1)}, u32[]{:S(2)}, u32[]{:S(2)}) collective-permute-start(f32[16,384]{1,0:T(8,128)S(1)} %concatenate.19), channel_id=1, source_target_pairs={{4,0},{8,12},{5,1},{9,13},{6,2},{10,14},{7,3},{11,15},{20,16},{24,... | collective-permute-start | bytes 73736 | tf_op jit(solution)/shard_map/ppermute | solution.py:662
  42.7 25.8 %collective-permute-done.4 = f32[16,384]{1,0:T(8,128)S(1)} collective-permute-done((f32[16,384]{1,0:T(8,128)S(1)}, f32[16,384]{1,0:T(8,128)S(1)}, u32[]{:S(2)}, u32[]{:S(2)}) %collective-permute-start.4) | collective-permute-done | bytes 24608 | tf_op jit(solution)/shard_map/ppermute | solution.py:662
  68.5 1.7 %shard_map.42 = f32[2,8,384]{2,1,0:T(8,128)} custom-call(f32[8,384]{1,0:T(8,128)S(1)} %get-tuple-element.38.value_v, f32[8,384]{1,0:T(8,128)S(1)} %get-tuple-element.37.value_u, f32[192,384]{1,0:T(8,128)S(1)} %get-tuple-element.27.kept_v, f32[8,384]{1,0:T(8,128)S(1)} %get-tuple-element.28.kept_b, f32[192,384]{1,0:T(8,128)S(1)} %get-tuple-element.29.kept_u, ...), custom_call_target="tpu_custom_call" | custom-call | tf_op jit(solution)/shard_map/pallas_call | solution.py:562
  (6 shorter events, 0.1 us)
Async XLA Ops:
  0.0 1.8 %copy-start.2 = (f32[2,96,384]{2,1,0:T(8,128)S(1)}, f32[2,96,384]{2,1,0:T(8,128)}, u32[]{:S(2)}) copy-start(f32[2,96,384]{2,1,0:T(8,128)} %param.3) | copy-start | bytes 884740
  1.1 9.5 %collective-permute-start.2 = (f32[192,384]{1,0:T(8,128)S(1)}, f32[192,384]{1,0:T(8,128)S(1)}, u32[]{:S(2)}, u32[]{:S(2)}) collective-permute-start(f32[192,384]{1,0:T(8,128)S(1)} %get-tuple-element.33), channel_id=1, source_target_pairs={{8,4},{12,8},{9,5},{13,9},{10,6},{14,10},{11,7},{15,11},{24,20},{2... | collective-permute-start | bytes 884744 | tf_op jit(solution)/shard_map/ppermute | solution.py:608
  1.8 8.8 %copy-start.1 = (f32[2,192,384]{2,1,0:T(8,128)S(1)}, f32[2,192,384]{2,1,0:T(8,128)}, u32[]{:S(2)}) copy-start(f32[2,192,384]{2,1,0:T(8,128)} %param.4) | copy-start | bytes 1769476
  1.9 6.9 %collective-permute-start = (f32[96,384]{1,0:T(8,128)S(1)}, f32[96,384]{1,0:T(8,128)S(1)}, u32[]{:S(2)}, u32[]{:S(2)}) collective-permute-start(f32[96,384]{1,0:T(8,128)S(1)} %get-tuple-element.36), channel_id=1, source_target_pairs={{0,2},{2,0},{1,3},{3,1},{4,6},{6,4},{5,7},{7,5},{8,10},{10,8},{9,1... | collective-permute-start | bytes 442376 | tf_op jit(solution)/shard_map/ppermute | solution.py:585
  8.8 1.9 %copy-start = (f32[2,8,384]{2,1,0:T(8,128)S(1)}, f32[2,8,384]{2,1,0:T(8,128)}, u32[]{:S(2)}) copy-start(f32[2,8,384]{2,1,0:T(8,128)} %loads.3) | copy-start | bytes 73732
  8.8 12.1 %collective-permute-start.1 = (f32[96,384]{1,0:T(8,128)S(1)}, f32[96,384]{1,0:T(8,128)S(1)}, u32[]{:S(2)}, u32[]{:S(2)}) collective-permute-start(f32[96,384]{1,0:T(8,128)S(1)} %get-tuple-element.18), channel_id=1, source_target_pairs={{0,2},{2,0},{1,3},{3,1},{4,6},{6,4},{5,7},{7,5},{8,10},{10,8},{9,1... | collective-permute-start | bytes 442376 | tf_op jit(solution)/shard_map/ppermute | solution.py:585
  21.0 11.8 %collective-permute-start.3 = (f32[200,384]{1,0:T(8,128)S(1)}, f32[200,384]{1,0:T(8,128)S(1)}, u32[]{:S(2)}, u32[]{:S(2)}) collective-permute-start(f32[200,384]{1,0:T(8,128)S(1)} %shard_map.38.own_v), channel_id=1, source_target_pairs={{0,4},{12,8},{1,5},{13,9},{2,6},{14,10},{3,7},{15,11},{16,20},{28,... | collective-permute-start | bytes 921608 | tf_op jit(solution)/shard_map/ppermute | solution.py:634
  41.4 27.1 %collective-permute-start.4 = (f32[16,384]{1,0:T(8,128)S(1)}, f32[16,384]{1,0:T(8,128)S(1)}, u32[]{:S(2)}, u32[]{:S(2)}) collective-permute-start(f32[16,384]{1,0:T(8,128)S(1)} %concatenate.19), channel_id=1, source_target_pairs={{4,0},{8,12},{5,1},{9,13},{6,2},{10,14},{7,3},{11,15},{20,16},{24,... | collective-permute-start | bytes 73736 | tf_op jit(solution)/shard_map/ppermute | solution.py:662

commit v3 on v2

v3 whole, which is shorter than its diff:
```python
import functools
import types

import jax
import jax.numpy as jnp
from jax import lax
from jax.sharding import PartitionSpec as P
from jax.experimental import pallas as pl
from jax.experimental.pallas import tpu as pltpu

HALF = 64
LANES = 2 * HALF


def dot(left, right, dims=((1,), (0,))):
    return lax.dot_general(
        left,
        right,
        (dims, ((), ())),
        precision=lax.Precision.HIGHEST,
        preferred_element_type=jnp.float32,
    )


def dot_flipped(left, right):
    return dot(left, right, ((1,), (1,)))


def lane_sign(shape):
    lane = lax.broadcasted_iota(jnp.int32, shape, 1)
    return jnp.where(lane % LANES < HALF, -1.0, 1.0).astype(jnp.float32)


def times_i(rows):
    pieces = [
        pltpu.roll(rows[:, start : start + LANES], HALF, 1)
        for start in range(0, rows.shape[1], LANES)
    ]
    turned = pieces[0] if len(pieces) == 1 else jnp.concatenate(pieces, axis=1)
    return turned * lane_sign(turned.shape)


def interleave(rows):
    count = rows.shape[1] // LANES
    pieces = []
    for chunk in range(count):
        pieces.append(rows[:, chunk * HALF : (chunk + 1) * HALF])
        pieces.append(rows[:, (count + chunk) * HALF : (count + chunk + 1) * HALF])
    return jnp.concatenate(pieces, axis=1)


def separate(rows):
    count = rows.shape[1] // LANES
    pieces = [rows[:, 2 * chunk * HALF : (2 * chunk + 1) * HALF] for chunk in range(count)]
    pieces += [rows[:, (2 * chunk + 1) * HALF : (2 * chunk + 2) * HALF] for chunk in range(count)]
    return jnp.concatenate(pieces, axis=1)


def embed(rows):
    turned = times_i(rows)
    pieces = []
    for start in range(0, rows.shape[0], HALF):
        pieces += [rows[start : start + HALF], turned[start : start + HALF]]
    return jnp.concatenate(pieces, axis=0)


def compact(embedded):
    return jnp.concatenate(
        [embedded[start : start + HALF] for start in range(0, embedded.shape[0], LANES)], axis=0
    )


GROUP = 16
TALL = 8


def product(left, right):
    return (left[0] * right[0] - left[1] * right[1], left[0] * right[1] + left[1] * right[0])


def minus(left, right):
    return (left[0] - right[0], left[1] - right[1])


def squared(value):
    return value[0] * value[0] + value[1] * value[1]


def spread_lane(rows, at):
    return jnp.broadcast_to(rows[:, at : at + 1], (TALL, LANES))


def pick(rows, at):
    return jnp.broadcast_to(rows[at : at + 1], (TALL, LANES))


def total(terms):
    while len(terms) > 1:
        terms = [sum(terms[i : i + 2][1:], terms[i]) for i in range(0, len(terms), 2)]
    return terms[0]


def spread_columns(part, step, count):
    return [(spread_lane(part, step + at), spread_lane(part, step + at + HALF)) for at in range(count)]


def invert_home(panel, spun, work, row_id):
    work = [tuple(jnp.where(row_id >= 0, half, 0.0) for half in value) for value in work]
    diagonal = pick(work[0][0], 0)
    for p in range(TALL):
        here = row_id == p
        real, imag = work[p]
        factor = 1.0 / diagonal
        across = {j: (pick(real, j), pick(imag, j)) for j in range(p + 1, TALL)}
        if p + 1 < TALL:
            diagonal = pick(work[p + 1][0], p + 1) - squared(across[p + 1]) * factor
        real = jnp.where(here, real - 1.0, real)
        imag = jnp.where(here, 0.0, imag)
        for j in range(p + 1, TALL):
            value = (across[j][0] * factor, across[j][1] * -factor)
            work[j] = minus(work[j], product((real, imag), value))
        row, turn = pick(panel, p) * factor, pick(spun, p) * factor
        panel = panel - (real * row + imag * turn)
        spun = spun - (real * turn - imag * row)
    return panel, spun


def invert_group(rows, first, sign, lane, row_id):
    above, below = rows[:TALL], rows[TALL:]
    inside = (lane % HALF >= first) & (lane % HALF < first + TALL)
    after = (lane % HALF >= first + TALL) & (lane % HALF < first + GROUP)
    home = spread_columns(above, first, TALL)
    side = spread_columns(below, first, TALL)
    panel = jnp.where(inside, 0.0, above)
    spun = pltpu.roll(panel, HALF, 1) * sign + jnp.where(lane == first + row_id + HALF, 1.0, 0.0)
    panel = panel + jnp.where(lane == first + row_id, 1.0, 0.0)
    panel, spun = invert_home(panel, spun, home, row_id)
    below = jnp.where(inside, 0.0, below) - total(
        [side[p][0] * pick(panel, p) + side[p][1] * pick(spun, p) for p in range(TALL)]
    )
    step = first + TALL
    home = spread_columns(below, step, TALL)
    side = spread_columns(panel, step, TALL)
    lower = jnp.where(after, 0.0, below)
    turned = pltpu.roll(lower, HALF, 1) * sign + jnp.where(lane == step + row_id + HALF, 1.0, 0.0)
    lower = lower + jnp.where(lane == step + row_id, 1.0, 0.0)
    lower, turned = invert_home(lower, turned, home, row_id)
    rows = [(pick(lower, p), pick(turned, p)) for p in range(TALL)]
    panel = jnp.where(after, 0.0, panel) - total(
        [side[p][0] * rows[p][0] + side[p][1] * rows[p][1] for p in range(TALL)]
    )
    spun = jnp.where(after, 0.0, spun) - total(
        [side[p][0] * rows[p][1] - side[p][1] * rows[p][0] for p in range(TALL)]
    )
    return jnp.concatenate([panel, lower], axis=0), jnp.concatenate([spun, turned], axis=0)


def spread_out(done, spun, first):
    last = HALF - first - GROUP
    before = [jnp.zeros((first, LANES), jnp.float32)] if first else []
    after = [jnp.zeros((last, LANES), jnp.float32)] if last else []
    return jnp.concatenate(before + [done] + after + before + [spun] + after, axis=0)


def invert_small(block, fillers=()):
    lane = lax.broadcasted_iota(jnp.int32, (1, LANES), 1)
    row_id = lax.broadcasted_iota(jnp.int32, (TALL, 1), 0)
    sign = lane_sign((1, LANES))
    group = block[:GROUP]
    fillers = list(fillers)
    slots = HALF // GROUP
    for first in range(0, HALF, GROUP):
        done, spun = invert_group(group, first, sign, lane, row_id)
        inside = (lane % HALF >= first) & (lane % HALF < first + GROUP)
        following = first + GROUP
        if following < HALF:
            parts = []
            for start in range(following, following + GROUP, TALL):
                old = block[start : start + TALL]
                columns = spread_columns(old, first, GROUP)
                parts.append(
                    jnp.where(inside, 0.0, old)
                    - total(
                        [
                            columns[at][0] * pick(done, at) + columns[at][1] * pick(spun, at)
                            for at in range(GROUP)
                        ]
                    )
                )
            group = jnp.concatenate(parts, axis=0)
        rest = jnp.where(inside, 0.0, block) - dot(
            jnp.where(inside, block, 0.0), spread_out(done, spun, first)
        )
        above = [rest[:first]] if first else []
        below = [rest[following:]] if following < HALF else []
        block = jnp.concatenate(above + [done] + below, axis=0)
        share = -(-len(fillers) // slots)
        for filler in fillers[:share]:
            filler()
        fillers, slots = fillers[share:], slots - 1
    return block


def doubled(rows):
    return jnp.concatenate([rows, times_i(rows)], axis=0)


def hermitian(block):
    return doubled(block).T[:HALF]


def chunk(rows, at):
    return rows[:, at * LANES : (at + 1) * LANES]


def chunks(rows):
    return [chunk(rows, at) for at in range(rows.shape[1] // LANES)]


def added(total_so_far, term):
    return term if total_so_far is None else total_so_far + term


def eliminate(count, block, tails, toward, before=None, keep=None):
    tails = list(tails)
    scaled = [None] * count
    lower = {}
    changes = {}
    sums = [None] * len(toward)
    pending = []

    def bulk(k, inverse, across, heads):
        def row_below(i):
            def run():
                lower[i, k] = dot(heads[i], inverse)
                change = dot(lower[i, k], across[:, (i - k - 1) * LANES :])
                for c in range(i, count):
                    changes[i, c] = added(changes.get((i, c)), chunk(change, c - i))

            return run

        def scale():
            scaled[k] = dot(tails[k], inverse)

        def shift():
            change = dot(scaled[k], across)
            for c in range(k + 1, count):
                tails[c] = tails[c] - chunk(change, c - k - 1)

        def gather(at):
            def run():
                (first, last), (low, high) = toward[at]
                term = dot_flipped(scaled[k][first:last], embed(tails[k][low:high]))
                sums[at] = added(sums[at], term)

            return run

        work = [row_below(i) for i in range(k + 2, count)] + [scale]
        if k + 1 < count:
            work.append(shift)
        return work + [gather(at) for at in range(len(toward))]

    for k in range(count):
        if before is not None:
            before(k)
        row = [
            block(k, c) - changes[k, c] if (k, c) in changes else block(k, c)
            for c in range(k, count)
        ]
        across, heads = None, {}
        if k + 1 < count:
            across = doubled(jnp.concatenate(row[1:], axis=1))
            heads = {i: hermitian(row[i - k]) for i in range(k + 1, count)}
        inverse = doubled(invert_small(row[0], pending))
        if k + 1 < count:
            lower[k + 1, k] = dot(heads[k + 1], inverse)
            change = dot(lower[k + 1, k], across)
            for c in range(k + 1, count):
                changes[k + 1, c] = added(changes.get((k + 1, c)), chunk(change, c - k - 1))
        if keep is not None:
            keep(k, inverse, across)
        pending = bulk(k, inverse, across, heads)
    for work in pending:
        work()
    stacked = [lower[i, k] for k in range(count) for i in range(k + 1, count)]
    return jnp.concatenate(scaled, axis=1), jnp.concatenate(stacked, axis=0), sums


def resolve(rows, lower):
    count = rows.shape[1] // LANES
    places = [(i, k) for k in range(count) for i in range(k + 1, count)]
    found = chunks(rows)
    for i in range(count - 1, 0, -1):
        for k in range(i):
            at = places.index((i, k)) * HALF
            found[k] = found[k] - dot(found[i], doubled(lower[at : at + HALF]))
    return jnp.concatenate(found, axis=1)


def blocks_of(*refs):
    def block(i, c):
        rows, lanes = slice(i * HALF, (i + 1) * HALF), slice(c * LANES, (c + 1) * LANES)
        value = refs[0][rows, lanes]
        for ref in refs[1:]:
            value = value + ref[rows, lanes]
        return value

    return block


def remote(source, target, send, receive, device):
    return pltpu.make_async_remote_copy(
        src_ref=source, dst_ref=target, send_sem=send, recv_sem=receive,
        device_id=device, device_id_type=pl.DeviceIdType.MESH,
    )


def siblings():
    size = lax.axis_size("rhs")
    return [{"rhs": lax.rem(lax.axis_index("rhs") + step, size)} for step in range(1, size)]


class Relay:
    def __init__(self, source, target, device, order, sems):
        self.source, self.target, self.device, self.order = source, target, device, order
        self.send, self.receive, self.pass_send, self.pass_receive = sems
        self.share = HALF // lax.axis_size("rhs")
        self.count = order // HALF

    def part(self, ref, core, piece):
        start = piece * HALF + core * self.share
        rows = pl.ds(pl.multiple_of(start, 8), self.share)
        return ref.at[rows, piece * LANES :]

    def copy(self, piece):
        if piece == self.count:
            after = pl.ds(self.order, self.source.shape[0] - self.order)
            source, target = self.source.at[after], self.target.at[after]
        else:
            core = lax.axis_index("rhs")
            source, target = (self.part(ref, core, piece) for ref in (self.source, self.target))
        return remote(
            source, target, self.send.at[piece], self.receive.at[piece], self.device
        )

    def passes(self, piece):
        part = self.part(self.target, lax.axis_index("rhs"), piece)
        return [
            remote(part, part, self.pass_send.at[piece, step], self.pass_receive.at[piece, step], to)
            for step, to in enumerate(siblings())
        ]

    def start(self):
        for piece in range(self.count + 1):
            self.copy(piece).start()

    def wait_sent(self):
        for piece in range(self.count + 1):
            self.copy(piece).wait_send()

    def wait_received(self):
        for piece in range(self.count):
            self.copy(piece).wait_recv()
            for copy in self.passes(piece):
                copy.start()
        self.copy(self.count).wait_recv()
        for piece in range(self.count):
            for copy in self.passes(piece):
                copy.wait()


def relay_semaphores(count):
    passing = (count, max(1, lax.axis_size("rhs") - 1))
    return [
        pltpu.SemaphoreType.DMA((count + 1,)), pltpu.SemaphoreType.DMA((count + 1,)),
        pltpu.SemaphoreType.DMA(passing), pltpu.SemaphoreType.DMA(passing),
    ]


def flipped_where(flip, ref, rows):
    @pl.when(flip)
    def _():
        ref[...] = compact(embed(rows).T)

    @pl.when(jnp.logical_not(flip))
    def _():
        ref[...] = rows


def reversed_where(flip, rows):
    pieces = chunks(rows)
    return jnp.where(flip, jnp.concatenate(pieces[::-1], axis=1), rows)


def solve_kernel(tree, diag, couplings, sources, result, *refs):
    at = types.SimpleNamespace(**jax.tree.unflatten(tree, refs))
    order, width = couplings.shape[1:]
    shard, rhs = diag.shape[1], sources.shape[1]
    count = order // HALF
    both = order + rhs
    slabs, orbs = lax.axis_size("slab"), lax.axis_size("orb")
    half = slabs // 2
    levels = half.bit_length() - 1
    slab, orb = lax.axis_index("slab"), lax.axis_index("orb")
    left = slab < half
    place = jnp.where(left, slab, slabs - 1 - slab)
    middle = place == half - 1
    inward = jnp.where(left, 1, -1)
    at_interior = jnp.where(left, 0, 1)
    paired = orbs == 2 and 2 * shard == 3 * HALF and order == 2 * shard
    turned = orb == 1 if paired else jnp.bool_(False)

    fetches = [
        pltpu.make_async_copy(ref, held, at.fetch.at[i])
        for i, (ref, held) in enumerate(((diag, at.diag), (sources, at.load), (couplings, at.coupling)))
    ]
    for fetch in fetches:
        fetch.start()
    barrier = pltpu.get_barrier_semaphore()

    def greet(device):
        pl.semaphore_signal(barrier, inc=1, device_id=device, device_id_type=pl.DeviceIdType.MESH)

    peers = [lax.rem(orb + step, orbs) for step in range(1, orbs)]
    owners = [lax.rem(orb + orbs - step, orbs) for step in range(1, orbs)]
    for device in [{"orb": peer} for peer in peers] + siblings():
        greet(device)
    expected = len(peers) + lax.axis_size("rhs") - 1
    for distance in sorted({1, *(2**level for level in range(levels))}):
        for other in (slab - distance, slab + distance):
            inside = (other >= 0) & (other < slabs)
            expected = expected + jnp.where(inside, 1, 0)
            pl.when(inside)(lambda other=other: greet({"slab": other}))
    fetches[0].wait()
    pl.semaphore_wait(barrier, expected)

    def rows_from(owner, low, size):
        return pl.ds(pl.multiple_of(owner * shard + low, 8), size)

    extra = shard - HALF
    if paired:
        def spans(owner):
            first = owner == 0
            return [(jnp.where(first, HALF, 0), extra), (jnp.where(first, 0, extra), HALF)]
    else:
        def spans(owner):
            return [(0, shard)]

    def gather_copies(gathered, layer, owner, step, device, first_sem, parts):
        return [
            remote(
                at.diag.at[layer, pl.ds(pl.multiple_of(low, 8), size)],
                gathered.at[rows_from(owner, low, size)],
                at.orb_send.at[first_sem + piece, step],
                at.orb_receive.at[first_sem + piece, step],
                device,
            )
            for piece, (low, size) in enumerate(parts)
        ]

    pieces = len(spans(orb))
    sent = []
    for step, peer in enumerate(peers):
        sent += gather_copies(
            at.interior, at_interior, orb, step, {"orb": peer}, 0, spans(orb)
        )
    for step, peer in enumerate(peers):
        sent += gather_copies(
            at.boundary, 1 - at_interior, orb, step, {"orb": peer}, pieces, [(0, shard)]
        )
    for copy in sent:
        copy.start()

    def wait_interior(piece):
        for step, owner in enumerate(owners):
            low, size = spans(owner)[piece]
            gather_copies(
                at.interior, at_interior, owner, step, {"orb": owner}, 0, spans(owner)
            )[piece].wait_recv()
            rows = rows_from(owner, low, size)
            at.pivot[rows] = interleave(at.interior[rows])

    def wait_boundary():
        for step, owner in enumerate(owners):
            gather_copies(
                at.boundary, 1 - at_interior, owner, step, {"orb": owner}, pieces, [(0, shard)]
            )[0].wait_recv()
        at.boundary[rows_from(orb, 0, shard)] = at.diag[1 - at_interior]

    fetches[1].wait()
    fetches[2].wait()
    shift = remote(
        at.coupling.at[0], at.shifted, at.shift.at[0], at.shift.at[1],
        {"slab": jnp.where(slab > 0, slab - 1, 1)},
    )
    shifts = slab >= half
    pl.when(shifts)(shift.start)

    def place_of(position):
        return jnp.where(turned, count - 1 - position, position)

    def pivot_block(i, c):
        rows = pl.ds(pl.multiple_of(place_of(i) * HALF, HALF), HALF)
        return at.pivot[rows, pl.ds(pl.multiple_of(place_of(c) * LANES, LANES), LANES)]

    at.pivot[rows_from(orb, 0, shard)] = interleave(at.diag[at_interior])
    flipped_where(left, at.to_v, interleave(at.coupling[1]))
    tail = jnp.concatenate([at.to_v[...], interleave(at.load[at_interior])], axis=0)

    def before(k):
        if paired and k > 0:
            wait_interior(k - 1)
        elif not paired and k == 0:
            wait_interior(0)

    def keep(k, inverse, across):
        at.inverse[k] = inverse
        if across is not None:
            at.across[k, :, : across.shape[1]] = across

    scaled, lower, sums = eliminate(
        count, pivot_block, chunks(reversed_where(turned, tail)), [((0, both), (0, order))],
        before, keep,
    )
    at.kept[:both] = scaled
    at.lower[...] = lower
    wait_boundary()
    own_v, own_u, cross = at.own_v, at.own_u, at.cross
    own_v[:order] = interleave(at.boundary[...]) - sums[0][:order]
    own_v[order:] = interleave(at.load[1 - at_interior]) - sums[0][order:]

    def relay(level, source, target, device):
        return Relay(source, target, device, order, at.relay[level])

    def outward():
        outer = at.outer

        @pl.when(left)
        def _():
            outer[...] = interleave(at.coupling[0])

        @pl.when(jnp.logical_not(left))
        def _():
            shift.wait_recv()
            outer[...] = compact(embed(interleave(at.shifted[...])).T)

        tails = chunks(reversed_where(turned, outer[...]))
        total_u = None
        for k in range(count):
            found = dot(tails[k], at.inverse[k])
            if k + 1 < count:
                change = dot(found, at.across[k, :, : (count - 1 - k) * LANES])
                for c in range(k + 1, count):
                    tails[c] = tails[c] - chunk(change, c - k - 1)
            lanes = slice(k * LANES, (k + 1) * LANES)
            at.kept[both:, lanes] = found
            stacked = jnp.concatenate([at.kept[:both, lanes], found], axis=0)
            total_u = added(total_u, dot_flipped(stacked, embed(tails[k])))
        own_u[:order] = -total_u[both:]
        own_u[order:] = -total_u[order:both]
        cross[...] = -total_u[:order]

    def no_outward():
        own_u[...] = jnp.zeros(own_u.shape, jnp.float32)
        cross[...] = jnp.zeros(cross.shape, jnp.float32)
        at.kept[both:] = jnp.zeros((order, width), jnp.float32)

    def settle():
        at.kept[...] = resolve(at.kept[...], at.lower[...])

    def settle_levels(below):
        for level in range(below):
            kept = at.level_kept[level]
            kept[...] = resolve(kept[...], at.level_lower[level][...])

    finish = []
    for level in range(levels):
        distance = 2**level
        wide = level < levels - 1
        sends = lax.rem(place, 2 * distance) == distance - 1
        takes = lax.rem(place, 2 * distance) == 2 * distance - 1
        device = {"slab": jnp.where(sends, slab + inward * distance, slab - inward * distance)}
        first_v = at.first_v[level]
        move = relay(level, own_v, first_v, device)
        pl.when(sends)(move.start)
        if level == 0:
            pl.when(place > 0)(outward)
            pl.when(place == 0)(no_outward)
        extras = []
        if wide:
            extras = [
                remote(
                    ref, target,
                    at.extra_send[level].at[i], at.extra_receive[level].at[i], device,
                )
                for i, (ref, target) in enumerate(
                    ((own_u, at.first_u[level]), (cross, at.first_cross[level]))
                )
            ]
            for copy in extras:
                pl.when(sends)(copy.start)
        kept, level_lower = at.level_kept[level], at.level_lower[level]

        @pl.when(sends)
        def _(level=level):
            settle()
            settle_levels(level)

        @pl.when(takes)
        def _(level=level, wide=wide, move=move, extras=extras, first_v=first_v, kept=kept, level_lower=level_lower):
            move.wait_received()
            for copy in extras:
                copy.wait_recv()
            load = first_v[order:] + own_u[order:]
            parts = [cross[...], load]
            toward = [((0, both), (0, order))]
            if wide:
                parts.append(compact(embed(at.first_cross[level][...]).T))
                toward.append(((0, both + order), (both, both + order)))
            tail = jnp.concatenate(parts, axis=0)
            scaled, lower, sums = eliminate(count, blocks_of(first_v, own_u), chunks(tail), toward)
            kept[...] = scaled
            level_lower[...] = lower
            own_v[...] = own_v[...] - sums[0]
            if wide:
                first_u = at.first_u[level]
                own_u[:order] = first_u[:order] - sums[1][both:]
                own_u[order:] = first_u[order:] - sums[1][order:both]
                cross[...] = -sums[1][:order]

        def sent_all(move=move, extras=extras):
            move.wait_sent()
            for copy in extras:
                copy.wait_send()

        finish.append((sends, sent_all))

    value_v, value_u = at.value_v, at.value_u
    value_u[...] = jnp.zeros(value_u.shape, jnp.float32)
    swap = relay(levels, own_v, at.other, {"slab": jnp.where(left, half, half - 1)})

    @pl.when(middle)
    def _():
        swap.start()
        settle_levels(levels)

        @pl.when(left)
        def _():
            shift.wait_recv()
            at.to_other[...] = interleave(at.shifted[...])

        @pl.when(jnp.logical_not(left))
        def _():
            at.to_other[...] = compact(embed(interleave(at.coupling[0])).T)

        settle()
        swap.wait_received()
        swap.wait_sent()
        other = at.other
        tail = jnp.concatenate([at.to_other[...], other[order:]], axis=0)
        _, _, sums = eliminate(count, blocks_of(other), chunks(tail), [((0, both), (0, order))])
        own_v[...] = own_v[...] - sums[0]
        scaled, lower, _ = eliminate(count, blocks_of(own_v), chunks(own_v[order:]), [])
        value_v[...] = resolve(scaled, lower)

    for level in range(levels - 1, -1, -1):
        distance = 2**level
        wide = level < levels - 1
        sends = lax.rem(place, 2 * distance) == 2 * distance - 1
        takes = lax.rem(place, 2 * distance) == distance - 1
        device = {"slab": jnp.where(takes, slab + inward * distance, slab - inward * distance)}
        back = remote(
            at.outbox[level], at.inbox[level],
            at.back.at[level, 0], at.back.at[level, 1], device,
        )

        @pl.when(sends)
        def _(level=level, wide=wide, back=back):
            kept, box = at.level_kept[level], at.outbox[level]
            found = kept[order:both] - dot(value_v[...], embed(kept[:order]))
            if wide:
                found = found - dot(value_u[...], embed(kept[both:]))
            box[rhs:] = value_u[...]
            box[:rhs] = found
            back.start()
            value_u[...] = found

        @pl.when(takes)
        def _(level=level, back=back):
            back.wait_recv()
            value_v[...] = at.inbox[level][:rhs]
            value_u[...] = at.inbox[level][rhs:]

        finish.append((sends, back.wait_send))

    kept = at.kept
    found = (
        kept[order:both]
        - dot(value_v[...], embed(kept[:order]))
        - dot(value_u[...], embed(kept[both:]))
    )
    result[at_interior] = separate(reversed_where(turned, found))
    result[1 - at_interior] = separate(value_v[...])
    for copy in sent:
        copy.wait_send()
    pl.when(shifts)(shift.wait_send)
    for condition, run in finish:
        pl.when(condition)(run)


def local(diag_blocks, couplings, sources):
    order, width = couplings.shape[1:]
    shard, rhs = diag_blocks.shape[1], sources.shape[1]
    count = order // HALF
    slabs, orbs = lax.axis_size("slab"), lax.axis_size("orb")
    levels = (slabs // 2).bit_length() - 1
    both = order + rhs
    square, tall, thin, lower = (
        (order, width), (both, width), (rhs, width), (count * (count - 1) // 2 * HALF, LANES),
    )
    dma = pltpu.SemaphoreType.DMA
    wide = (both + order, width)

    def vmem(*shape):
        return pltpu.VMEM(shape, jnp.float32)

    scratch = dict(
        diag=vmem(2, shard, width), load=vmem(2, rhs, width), coupling=vmem(2, order, width),
        interior=vmem(*square), boundary=vmem(*square), shifted=vmem(*square), pivot=vmem(*square),
        to_v=vmem(*square), outer=vmem(*square), kept=vmem(*wide), lower=vmem(*lower),
        inverse=vmem(count, LANES, LANES), across=vmem(count, LANES, (count - 1) * LANES),
        own_v=vmem(*tall), own_u=vmem(*tall), cross=vmem(*square), other=vmem(*tall),
        to_other=vmem(*square), value_v=vmem(*thin), value_u=vmem(*thin),
        fetch=dma((3,)), shift=dma((2,)), back=dma((max(1, levels), 2)),
        orb_send=dma((3, max(1, orbs - 1))), orb_receive=dma((3, max(1, orbs - 1))),
        relay=[relay_semaphores(count) for _ in range(levels + 1)],
        first_v=[vmem(*tall) for _ in range(levels)],
        level_kept=[vmem(*wide) if level < levels - 1 else vmem(*tall) for level in range(levels)],
        level_lower=[vmem(*lower) for _ in range(levels)],
        outbox=[vmem(2 * rhs, width) for _ in range(levels)],
        inbox=[vmem(2 * rhs, width) for _ in range(levels)],
        first_u=[vmem(*tall) for _ in range(levels - 1)],
        first_cross=[vmem(*square) for _ in range(levels - 1)],
        extra_send=[dma((2,)) for _ in range(levels - 1)],
        extra_receive=[dma((2,)) for _ in range(levels - 1)],
    )
    leaves, tree = jax.tree.flatten(scratch)
    return pl.pallas_call(
        functools.partial(solve_kernel, tree),
        out_shape=jax.ShapeDtypeStruct(sources.shape, jnp.float32),
        in_specs=[pl.BlockSpec(memory_space=pl.ANY)] * 3,
        out_specs=pl.BlockSpec(memory_space=pltpu.VMEM),
        scratch_shapes=leaves,
        compiler_params=pltpu.CompilerParams(
            vmem_limit_bytes=67043328, collective_id=0, has_side_effects=True
        ),
    )(diag_blocks, couplings, sources)


def solution(mesh):
    placed = (
        P(("energy", "slab"), "orb", None),
        P(("energy", "slab"), None, None),
        P(("energy", "slab"), ("orb", "rhs"), None),
    )
    return jax.shard_map(
        local,
        mesh=mesh,
        in_specs=placed,
        out_specs=P(("energy", "slab"), ("orb", "rhs"), None),
        check_vma=False,
    )
```

time: 70.4 us -> 53 us (0.75)
  waiting for transfers between devices: 35.1 us -> 0 us
  Pallas kernels: 20.5 us -> 51.5 us
  starting transfers between devices: 13.1 us -> 0 us
    ppermute x5 -> x0, waiting for transfers between devices: 35.1 us -> none  [the longest x1 25.8 us: local(): lax.ppermute(jnp.concatenate([middle, value_u]), 'slab', [(b, a) for a, b...]
    pallas_call x6 -> x1, Pallas kernels: 20.5 us -> 51.5 us  [local(): pl.pallas_call(functools.partial(solve_kernel, tree), out_shape=jax.Shape...]
    ppermute x5 -> x0, starting transfers between devices: 13.1 us -> none  [the longest x1 6.32 us: local(): first_v = lax.ppermute(new_v, 'slab', pairs)]
    unnamed x6 -> x1, local copies, waits for them, and re-layouts: 0.02 us -> 1.35 us
    squeeze x1 -> x0, local copies, waits for them, and re-layouts: 1.13 us -> none  [local(): outer = jnp.where(left, jnp.where(slab > 0, couplings[0], 0.0), shifted)]
  transfers between devices with their start and end apart: 5 -> 0, of which waited for: 3 -> 0; matrix products, arithmetic and copies ran while one was open for 0% -> 0% of each run, Pallas kernels for 14% -> 0%
where the time goes in v3:
time: 53 us; the launch traced here: 52.8 us
  Pallas kernels  51.5 us (97%)
  local copies, waits for them, and re-layouts  1.35 us (3%)
    pallas_call x1, Pallas kernels, local(): pl.pallas_call(functools.partial(solve_kernel, tree), out_shape=jax.Shape...  51.5 us
    unnamed x1, local copies, waits for them, and re-layouts  1.35 us

profile of v3, /device:TPU:0, one launch (start us, length us, event | category | flops | bytes accessed | tf_op | source)
XLA Modules:
  0.0 52.8 jit_solution(1026287291740428224)
XLA Ops:
  0.0 51.5 %shard_map.37 = f32[2,8,384]{2,1,0:T(8,128)} custom-call(f32[2,96,384]{2,1,0:T(8,128)} %diag.1, f32[2,192,384]{2,1,0:T(8,128)} %couplings.1, f32[2,8,384]{2,1,0:T(8,128)} %sources.1), custom_call_target="tpu_custom_call" | custom-call | tf_op jit(solution)/shard_map/pallas_call | solution.py:748
  51.5 1.3 %copy.5 = f32[2,8,384]{2,1,0:T(8,128)} copy(f32[2,8,384]{2,1,0:T(8,128)} %shard_map.37) | data formatting | bytes 49152

commit v4 on v3

--- a/solution.py
+++ b/solution.py
@@ -221,8 +221,8 @@
     return term if total_so_far is None else total_so_far + term
 
 
-def eliminate(count, block, tails, toward, before=None, keep=None):
-    tails = list(tails)
+def eliminate(count, block, make_tails, toward, before=None, keep=None, after=None):
+    tails = []
     scaled = [None] * count
     lower = {}
     changes = {}
@@ -260,18 +260,22 @@
             work.append(shift)
         return work + [gather(at) for at in range(len(toward))]
 
+    def current(i, c):
+        return block(i, c) - changes[i, c] if (i, c) in changes else block(i, c)
+
     for k in range(count):
         if before is not None:
             before(k)
-        row = [
-            block(k, c) - changes[k, c] if (k, c) in changes else block(k, c)
-            for c in range(k, count)
-        ]
+        if k == min(1, count - 1):
+            tails.extend(make_tails())
+        inverse = doubled(invert_small(current(k, k), pending))
+        if after is not None:
+            after(k)
         across, heads = None, {}
         if k + 1 < count:
-            across = doubled(jnp.concatenate(row[1:], axis=1))
-            heads = {i: hermitian(row[i - k]) for i in range(k + 1, count)}
-        inverse = doubled(invert_small(row[0], pending))
+            right = [current(k, c) for c in range(k + 1, count)]
+            across = doubled(jnp.concatenate(right, axis=1))
+            heads = {i: hermitian(right[i - k - 1]) for i in range(k + 1, count)}
         if k + 1 < count:
             lower[k + 1, k] = dot(heads[k + 1], inverse)
             change = dot(lower[k + 1, k], across)
@@ -315,66 +319,60 @@
     )
 
 
-def siblings():
-    size = lax.axis_size("rhs")
-    return [{"rhs": lax.rem(lax.axis_index("rhs") + step, size)} for step in range(1, size)]
-
-
-class Relay:
+class Move:
     def __init__(self, source, target, device, order, sems):
-        self.source, self.target, self.device, self.order = source, target, device, order
-        self.send, self.receive, self.pass_send, self.pass_receive = sems
-        self.share = HALF // lax.axis_size("rhs")
+        self.source, self.target, self.device = source, target, device
+        self.send, self.receive = sems
         self.count = order // HALF
-
-    def part(self, ref, core, piece):
-        start = piece * HALF + core * self.share
-        rows = pl.ds(pl.multiple_of(start, 8), self.share)
-        return ref.at[rows, piece * LANES :]
-
-    def copy(self, piece):
-        if piece == self.count:
-            after = pl.ds(self.order, self.source.shape[0] - self.order)
-            source, target = self.source.at[after], self.target.at[after]
-        else:
-            core = lax.axis_index("rhs")
-            source, target = (self.part(ref, core, piece) for ref in (self.source, self.target))
+        self.loads_at = min(1, self.count - 1)
+        self.load = pl.ds(order, source.shape[0] - order)
+
+    def copy(self, at, rows, lanes):
         return remote(
-            source, target, self.send.at[piece], self.receive.at[piece], self.device
+            self.source.at[rows, lanes], self.target.at[rows, lanes],
+            self.send.at[at], self.receive.at[at], self.device,
         )
 
-    def passes(self, piece):
-        part = self.part(self.target, lax.axis_index("rhs"), piece)
-        return [
-            remote(part, part, self.pass_send.at[piece, step], self.pass_receive.at[piece, step], to)
-            for step, to in enumerate(siblings())
-        ]
+    def own(self, i):
+        return self.copy(2 * i, pl.ds(i * HALF, HALF), pl.ds(i * LANES, LANES))
+
+    def right(self, i):
+        size = (self.count - 1 - i) * LANES
+        return self.copy(2 * i + 1, pl.ds(i * HALF, HALF), pl.ds((i + 1) * LANES, size))
+
+    def tail(self):
+        return self.copy(2 * self.count, self.load, pl.ds(0, self.source.shape[1]))
+
+    def copies(self):
+        found = []
+        for i in range(self.count):
+            found.append(self.own(i))
+            if i == self.loads_at:
+                found.append(self.tail())
+            if i + 1 < self.count:
+                found.append(self.right(i))
+        return found
 
     def start(self):
-        for piece in range(self.count + 1):
-            self.copy(piece).start()
+        for copy in self.copies():
+            copy.start()
 
     def wait_sent(self):
-        for piece in range(self.count + 1):
-            self.copy(piece).wait_send()
-
-    def wait_received(self):
-        for piece in range(self.count):
-            self.copy(piece).wait_recv()
-            for copy in self.passes(piece):
-                copy.start()
-        self.copy(self.count).wait_recv()
-        for piece in range(self.count):
-            for copy in self.passes(piece):
-                copy.wait()
-
-
-def relay_semaphores(count):
-    passing = (count, max(1, lax.axis_size("rhs") - 1))
-    return [
-        pltpu.SemaphoreType.DMA((count + 1,)), pltpu.SemaphoreType.DMA((count + 1,)),
-        pltpu.SemaphoreType.DMA(passing), pltpu.SemaphoreType.DMA(passing),
-    ]
+        for copy in self.copies():
+            copy.wait_send()
+
+    def before(self, k):
+        self.own(k).wait_recv()
+        if k == self.loads_at:
+            self.tail().wait_recv()
+
+    def after(self, k):
+        if k + 1 < self.count:
+            self.right(k).wait_recv()
+
+
+def move_semaphores(count):
+    return [pltpu.SemaphoreType.DMA((2 * count + 1,)) for _ in range(2)]
 
 
 def flipped_where(flip, ref, rows):
@@ -412,7 +410,7 @@
 
     fetches = [
         pltpu.make_async_copy(ref, held, at.fetch.at[i])
-        for i, (ref, held) in enumerate(((diag, at.diag), (sources, at.load), (couplings, at.coupling)))
+        for i, (ref, held) in enumerate(((diag, at.diag), (couplings, at.coupling)))
     ]
     for fetch in fetches:
         fetch.start()
@@ -423,9 +421,9 @@
 
     peers = [lax.rem(orb + step, orbs) for step in range(1, orbs)]
     owners = [lax.rem(orb + orbs - step, orbs) for step in range(1, orbs)]
-    for device in [{"orb": peer} for peer in peers] + siblings():
+    for device in [{"orb": peer} for peer in peers]:
         greet(device)
-    expected = len(peers) + lax.axis_size("rhs") - 1
+    expected = len(peers)
     for distance in sorted({1, *(2**level for level in range(levels))}):
         for other in (slab - distance, slab + distance):
             inside = (other >= 0) & (other < slabs)
@@ -488,7 +486,6 @@
         at.boundary[rows_from(orb, 0, shard)] = at.diag[1 - at_interior]
 
     fetches[1].wait()
-    fetches[2].wait()
     shift = remote(
         at.coupling.at[0], at.shifted, at.shift.at[0], at.shift.at[1],
         {"slab": jnp.where(slab > 0, slab - 1, 1)},
@@ -505,7 +502,7 @@
 
     at.pivot[rows_from(orb, 0, shard)] = interleave(at.diag[at_interior])
     flipped_where(left, at.to_v, interleave(at.coupling[1]))
-    tail = jnp.concatenate([at.to_v[...], interleave(at.load[at_interior])], axis=0)
+    tail = jnp.concatenate([at.to_v[...], interleave(sources[at_interior])], axis=0)
 
     def before(k):
         if paired and k > 0:
@@ -519,7 +516,7 @@
             at.across[k, :, : across.shape[1]] = across
 
     scaled, lower, sums = eliminate(
-        count, pivot_block, chunks(reversed_where(turned, tail)), [((0, both), (0, order))],
+        count, pivot_block, lambda: chunks(reversed_where(turned, tail)), [((0, both), (0, order))],
         before, keep,
     )
     at.kept[:both] = scaled
@@ -527,10 +524,10 @@
     wait_boundary()
     own_v, own_u, cross = at.own_v, at.own_u, at.cross
     own_v[:order] = interleave(at.boundary[...]) - sums[0][:order]
-    own_v[order:] = interleave(at.load[1 - at_interior]) - sums[0][order:]
-
-    def relay(level, source, target, device):
-        return Relay(source, target, device, order, at.relay[level])
+    own_v[order:] = interleave(sources[1 - at_interior]) - sums[0][order:]
+
+    def moved(level, source, target, device):
+        return Move(source, target, device, order, at.moves[level])
 
     def outward():
         outer = at.outer
@@ -581,7 +578,7 @@
         takes = lax.rem(place, 2 * distance) == 2 * distance - 1
         device = {"slab": jnp.where(sends, slab + inward * distance, slab - inward * distance)}
         first_v = at.first_v[level]
-        move = relay(level, own_v, first_v, device)
+        move = moved(level, own_v, first_v, device)
         pl.when(sends)(move.start)
         if level == 0:
             pl.when(place > 0)(outward)
@@ -608,17 +605,21 @@
 
         @pl.when(takes)
         def _(level=level, wide=wide, move=move, extras=extras, first_v=first_v, kept=kept, level_lower=level_lower):
-            move.wait_received()
-            for copy in extras:
-                copy.wait_recv()
-            load = first_v[order:] + own_u[order:]
-            parts = [cross[...], load]
             toward = [((0, both), (0, order))]
             if wide:
-                parts.append(compact(embed(at.first_cross[level][...]).T))
                 toward.append(((0, both + order), (both, both + order)))
-            tail = jnp.concatenate(parts, axis=0)
-            scaled, lower, sums = eliminate(count, blocks_of(first_v, own_u), chunks(tail), toward)
+
+            def tails():
+                parts = [cross[...], first_v[order:] + own_u[order:]]
+                for copy in extras:
+                    copy.wait_recv()
+                if wide:
+                    parts.append(compact(embed(at.first_cross[level][...]).T))
+                return chunks(jnp.concatenate(parts, axis=0))
+
+            scaled, lower, sums = eliminate(
+                count, blocks_of(first_v, own_u), tails, toward, before=move.before, after=move.after
+            )
             kept[...] = scaled
             level_lower[...] = lower
             own_v[...] = own_v[...] - sums[0]
@@ -637,7 +638,7 @@
 
     value_v, value_u = at.value_v, at.value_u
     value_u[...] = jnp.zeros(value_u.shape, jnp.float32)
-    swap = relay(levels, own_v, at.other, {"slab": jnp.where(left, half, half - 1)})
+    swap = moved(levels, own_v, at.other, {"slab": jnp.where(left, half, half - 1)})
 
     @pl.when(middle)
     def _():
@@ -653,14 +654,22 @@
         def _():
             at.to_other[...] = compact(embed(interleave(at.coupling[0])).T)
 
-        settle()
-        swap.wait_received()
-        swap.wait_sent()
         other = at.other
-        tail = jnp.concatenate([at.to_other[...], other[order:]], axis=0)
-        _, _, sums = eliminate(count, blocks_of(other), chunks(tail), [((0, both), (0, order))])
-        own_v[...] = own_v[...] - sums[0]
-        scaled, lower, _ = eliminate(count, blocks_of(own_v), chunks(own_v[order:]), [])
+
+        def swapped(k):
+            swap.before(k)
+            if k == count - 1:
+                swap.wait_sent()
+
+        _, _, sums = eliminate(
+            count, blocks_of(other),
+            lambda: chunks(jnp.concatenate([at.to_other[...], other[order:]], axis=0)),
+            [((0, both), (0, order))], before=swapped, after=swap.after,
+        )
+        reduced = own_v[...] - sums[0]
+        scaled, lower, _ = eliminate(
+            count, blocks_of(reduced), lambda: chunks(reduced[order:]), []
+        )
         value_v[...] = resolve(scaled, lower)
 
     for level in range(levels - 1, -1, -1):
@@ -699,7 +708,15 @@
         - dot(value_v[...], embed(kept[:order]))
         - dot(value_u[...], embed(kept[both:]))
     )
-    result[at_interior] = separate(reversed_where(turned, found))
+
+    @pl.when(middle)
+    def _():
+        result[at_interior] = separate(reversed_where(turned, resolve(found, at.lower[...])))
+
+    @pl.when(jnp.logical_not(middle))
+    def _():
+        result[at_interior] = separate(reversed_where(turned, found))
+
     result[1 - at_interior] = separate(value_v[...])
     for copy in sent:
         copy.wait_send()
@@ -725,15 +742,15 @@
         return pltpu.VMEM(shape, jnp.float32)
 
     scratch = dict(
-        diag=vmem(2, shard, width), load=vmem(2, rhs, width), coupling=vmem(2, order, width),
+        diag=vmem(2, shard, width), coupling=vmem(2, order, width),
         interior=vmem(*square), boundary=vmem(*square), shifted=vmem(*square), pivot=vmem(*square),
         to_v=vmem(*square), outer=vmem(*square), kept=vmem(*wide), lower=vmem(*lower),
         inverse=vmem(count, LANES, LANES), across=vmem(count, LANES, (count - 1) * LANES),
         own_v=vmem(*tall), own_u=vmem(*tall), cross=vmem(*square), other=vmem(*tall),
         to_other=vmem(*square), value_v=vmem(*thin), value_u=vmem(*thin),
-        fetch=dma((3,)), shift=dma((2,)), back=dma((max(1, levels), 2)),
+        fetch=dma((2,)), shift=dma((2,)), back=dma((max(1, levels), 2)),
         orb_send=dma((3, max(1, orbs - 1))), orb_receive=dma((3, max(1, orbs - 1))),
-        relay=[relay_semaphores(count) for _ in range(levels + 1)],
+        moves=[move_semaphores(count) for _ in range(levels + 1)],
         first_v=[vmem(*tall) for _ in range(levels)],
         level_kept=[vmem(*wide) if level < levels - 1 else vmem(*tall) for level in range(levels)],
         level_lower=[vmem(*lower) for _ in range(levels)],
@@ -748,11 +765,11 @@
     return pl.pallas_call(
         functools.partial(solve_kernel, tree),
         out_shape=jax.ShapeDtypeStruct(sources.shape, jnp.float32),
-        in_specs=[pl.BlockSpec(memory_space=pl.ANY)] * 3,
+        in_specs=[pl.BlockSpec(memory_space=space) for space in (pl.ANY, pl.ANY, pltpu.VMEM)],
         out_specs=pl.BlockSpec(memory_space=pltpu.VMEM),
         scratch_shapes=leaves,
         compiler_params=pltpu.CompilerParams(
-            vmem_limit_bytes=67043328, collective_id=0, has_side_effects=True
+            vmem_limit_bytes=67043328 - 131072, collective_id=0, has_side_effects=True
         ),
     )(diag_blocks, couplings, sources)
 

time: 53 us -> 50.9 us (0.960)
  Pallas kernels: 51.5 us -> 49.3 us
    pallas_call x1, Pallas kernels: 51.5 us -> 49.3 us  [local(): pl.pallas_call(functools.partial(solve_kernel, tree), out_shape=jax.Shape...]
where the time goes in v4:
time: 50.9 us; the launch traced here: 50.7 us
  Pallas kernels  49.3 us (97%)
  local copies, waits for them, and re-layouts  1.35 us (3%)
    pallas_call x1, Pallas kernels, local(): pl.pallas_call(functools.partial(solve_kernel, tree), out_shape=jax.Shape...  49.3 us
    unnamed x1, local copies, waits for them, and re-layouts  1.35 us

profile of v4, /device:TPU:0, one launch (start us, length us, event | category | flops | bytes accessed | tf_op | source)
XLA Modules:
  0.0 50.7 jit_solution(576756725897262688)
XLA Ops:
  0.0 49.3 %shard_map.37 = f32[2,8,384]{2,1,0:T(8,128)} custom-call(f32[2,96,384]{2,1,0:T(8,128)} %diag.1, f32[2,192,384]{2,1,0:T(8,128)} %couplings.1, f32[2,8,384]{2,1,0:T(8,128)} %sources.1), custom_call_target="tpu_custom_call" | custom-call | tf_op jit(solution)/shard_map/pallas_call | solution.py:765
  49.3 1.3 %copy.5 = f32[2,8,384]{2,1,0:T(8,128)} copy(f32[2,8,384]{2,1,0:T(8,128)} %shard_map.37) | data formatting | bytes 49152

commit v5 on v4

--- a/solution.py
+++ b/solution.py
@@ -410,7 +410,7 @@
 
     fetches = [
         pltpu.make_async_copy(ref, held, at.fetch.at[i])
-        for i, (ref, held) in enumerate(((diag, at.diag), (couplings, at.coupling)))
+        for i, (ref, held) in enumerate(((diag, at.diag), (couplings, at.coupling), (sources, at.load)))
     ]
     for fetch in fetches:
         fetch.start()
@@ -486,6 +486,7 @@
         at.boundary[rows_from(orb, 0, shard)] = at.diag[1 - at_interior]
 
     fetches[1].wait()
+    fetches[2].wait()
     shift = remote(
         at.coupling.at[0], at.shifted, at.shift.at[0], at.shift.at[1],
         {"slab": jnp.where(slab > 0, slab - 1, 1)},
@@ -501,22 +502,26 @@
         return at.pivot[rows, pl.ds(pl.multiple_of(place_of(c) * LANES, LANES), LANES)]
 
     at.pivot[rows_from(orb, 0, shard)] = interleave(at.diag[at_interior])
-    flipped_where(left, at.to_v, interleave(at.coupling[1]))
-    tail = jnp.concatenate([at.to_v[...], interleave(sources[at_interior])], axis=0)
 
     def before(k):
+        if k == min(1, count - 1):
+            flipped_where(left, at.to_v, interleave(at.coupling[1]))
         if paired and k > 0:
             wait_interior(k - 1)
         elif not paired and k == 0:
             wait_interior(0)
 
+    def interior_tails():
+        tail = jnp.concatenate([at.to_v[...], interleave(at.load[at_interior])], axis=0)
+        return chunks(reversed_where(turned, tail))
+
     def keep(k, inverse, across):
         at.inverse[k] = inverse
         if across is not None:
             at.across[k, :, : across.shape[1]] = across
 
     scaled, lower, sums = eliminate(
-        count, pivot_block, lambda: chunks(reversed_where(turned, tail)), [((0, both), (0, order))],
+        count, pivot_block, interior_tails, [((0, both), (0, order))],
         before, keep,
     )
     at.kept[:both] = scaled
@@ -524,7 +529,7 @@
     wait_boundary()
     own_v, own_u, cross = at.own_v, at.own_u, at.cross
     own_v[:order] = interleave(at.boundary[...]) - sums[0][:order]
-    own_v[order:] = interleave(sources[1 - at_interior]) - sums[0][order:]
+    own_v[order:] = interleave(at.load[1 - at_interior]) - sums[0][order:]
 
     def moved(level, source, target, device):
         return Move(source, target, device, order, at.moves[level])
@@ -742,13 +747,13 @@
         return pltpu.VMEM(shape, jnp.float32)
 
     scratch = dict(
-        diag=vmem(2, shard, width), coupling=vmem(2, order, width),
+        diag=vmem(2, shard, width), coupling=vmem(2, order, width), load=vmem(2, rhs, width),
         interior=vmem(*square), boundary=vmem(*square), shifted=vmem(*square), pivot=vmem(*square),
         to_v=vmem(*square), outer=vmem(*square), kept=vmem(*wide), lower=vmem(*lower),
         inverse=vmem(count, LANES, LANES), across=vmem(count, LANES, (count - 1) * LANES),
         own_v=vmem(*tall), own_u=vmem(*tall), cross=vmem(*square), other=vmem(*tall),
         to_other=vmem(*square), value_v=vmem(*thin), value_u=vmem(*thin),
-        fetch=dma((2,)), shift=dma((2,)), back=dma((max(1, levels), 2)),
+        fetch=dma((3,)), shift=dma((2,)), back=dma((max(1, levels), 2)),
         orb_send=dma((3, max(1, orbs - 1))), orb_receive=dma((3, max(1, orbs - 1))),
         moves=[move_semaphores(count) for _ in range(levels + 1)],
         first_v=[vmem(*tall) for _ in range(levels)],
@@ -762,16 +767,20 @@
         extra_receive=[dma((2,)) for _ in range(levels - 1)],
     )
     leaves, tree = jax.tree.flatten(scratch)
+
+    def held(array):
+        return pltpu.with_memory_space_constraint(array, pltpu.HBM)
+
     return pl.pallas_call(
         functools.partial(solve_kernel, tree),
         out_shape=jax.ShapeDtypeStruct(sources.shape, jnp.float32),
-        in_specs=[pl.BlockSpec(memory_space=space) for space in (pl.ANY, pl.ANY, pltpu.VMEM)],
+        in_specs=[pl.BlockSpec(memory_space=pl.ANY)] * 3,
         out_specs=pl.BlockSpec(memory_space=pltpu.VMEM),
         scratch_shapes=leaves,
         compiler_params=pltpu.CompilerParams(
-            vmem_limit_bytes=67043328 - 131072, collective_id=0, has_side_effects=True
+            vmem_limit_bytes=48 * 1024 * 1024, collective_id=0, has_side_effects=True
         ),
-    )(diag_blocks, couplings, sources)
+    )(held(diag_blocks), held(couplings), held(sources))
 
 
 def solution(mesh):

time: 50.9 us -> 48.8 us (0.959)
  Pallas kernels: 49.3 us -> 48 us
  local copies, waits for them, and re-layouts: 1.35 us -> 0.61 us
    pallas_call x1, Pallas kernels: 49.3 us -> 48 us  [local(): pl.pallas_call(functools.partial(solve_kernel, tree), out_shape=jax.Shape...]
    unnamed x1, local copies, waits for them, and re-layouts: 1.35 us -> 0.61 us
where the time goes in v5:
time: 48.8 us; the launch traced here: 48.6 us
  Pallas kernels  48 us (98%)
  local copies, waits for them, and re-layouts  0.61 us (1%)
    pallas_call x1, Pallas kernels, local(): pl.pallas_call(functools.partial(solve_kernel, tree), out_shape=jax.Shape...  48 us

profile of v5, /device:TPU:0, one launch (start us, length us, event | category | flops | bytes accessed | tf_op | source)
XLA Modules:
  0.0 48.6 jit_solution(18269763103012995971)
XLA Ops:
  0.0 48.0 %shard_map.37 = f32[2,8,384]{2,1,0:T(8,128)S(1)} custom-call(f32[2,96,384]{2,1,0:T(8,128)} %diag.1, f32[2,192,384]{2,1,0:T(8,128)} %couplings.1, f32[2,8,384]{2,1,0:T(8,128)} %sources.1), custom_call_target="tpu_custom_call" | custom-call | tf_op jit(solution)/shard_map/pallas_call | solution.py:774
  48.0 0.6 %copy.5 = f32[2,8,384]{2,1,0:T(8,128)} copy(f32[2,8,384]{2,1,0:T(8,128)S(1)} %shard_map.37) | data formatting | bytes 49152
